TPU v7x, 128 devices: a whole 4x4x4 slice. The times are simulated.
128 devices in a mesh: tm: 8 (over z, core), lat: 16 (over x, y).
Axes of the slice: x: 4, y: 4, z: 4, core: 2. Of those that a mesh axis runs over, the one named last changes fastest.
Arguments:
- frames: bfloat16 [256, 512, 1024], P('tm', 'lat'), may hold values from -6 to 6
- projection: bfloat16 [256, 512, 256], P(('tm', 'lat')), may hold values from -0.25 to 0.25
- degree_range: int32 [256, 2], replicated, may hold values from 0 to 256, as said below
- offsets: int32 [8], replicated, may hold values from 0 to 63
Outputs:
- coupling: bfloat16 [256, 2, 8, 256, 2, 256], P(('tm', 'lat'))
Inputs may be any that keep to these rules, and one draw needn't show every extreme that they name: `degree_range`: row m holds lo and hi with min(m, 255) <= lo < hi <= 256.
All inputs are finite; a program needn't handle non-finite values.
Results may differ from a plain program's by a relative error of at most 0.0093.
Values may be sent and summed in bfloat16 or wider, within the bound.
A program may use at most 64 MiB of HBM per device.

v0:
```python
import math

import jax
import jax.numpy as jnp
from jax import lax
from jax.sharding import PartitionSpec as P


def shifted_2(block, axis, distance):
    devices = range(lax.axis_size(axis))
    route = [(i - distance, i) for i in devices if i - distance in devices]
    return lax.ppermute(block, axis, route)


def longitude_table(lon_count, order_ids):
    longitude_points = jnp.arange(lon_count, dtype=jnp.int32)
    rotation_radians = longitude_points[:, None] * order_ids[None, :] % lon_count
    angle = rotation_radians.astype(jnp.float32) * (2.0 * math.pi / lon_count)
    factor = 1.0 / math.sqrt(lon_count)
    table = jnp.stack([jnp.cos(angle) * factor, -jnp.sin(angle) * factor], axis=2)
    return table.reshape(lon_count, -1).astype(jnp.bfloat16)


def time_table(entry_total):
    observation_epochs = jnp.arange(entry_total, dtype=jnp.int32)
    rotation_radians = observation_epochs[:, None] * observation_epochs[None, :] % entry_total
    angle = rotation_radians.astype(jnp.float32) * (2.0 * math.pi / entry_total)
    factor = 1.0 / math.sqrt(entry_total)
    cosine = jnp.cos(angle) * factor
    sine = jnp.sin(angle) * factor
    upper = jnp.concatenate([cosine, sine], axis=1)
    lower = jnp.concatenate([-sine, cosine], axis=1)
    return jnp.concatenate([upper, lower], axis=0).astype(jnp.bfloat16)


def couple(own, partners, offsets, frame_count):
    own_count, _, harmonic_degree_total = own.shape
    offset_count = offsets.shape[0]
    epochs = jnp.arange(frame_count, dtype=jnp.int32)
    source = (epochs[None, :, None] - offsets[:, None, None]) % frame_count
    selector = (epochs[None, None, :] == source).astype(jnp.bfloat16)
    halves = own.reshape(own_count, 2, frame_count, harmonic_degree_total)
    shifted = jnp.einsum("kwv,oqvl->okqwl", selector, halves, preferred_element_type=jnp.float32)
    shifted = shifted.astype(jnp.bfloat16).reshape(
        own_count, offset_count, 2 * frame_count, harmonic_degree_total
    )
    imag_part = jnp.concatenate(
        [partners[:, :, frame_count:], -partners[:, :, :frame_count]], axis=2
    )
    both = jnp.concatenate([partners, imag_part], axis=3)
    scale = 1.0 / math.sqrt(frame_count)
    results = []
    for partner_index in range(2):
        product = jnp.einsum(
            "okrl,orm->oklm", shifted, both[:, partner_index], preferred_element_type=jnp.float32
        )
        results.append((product * scale).astype(jnp.bfloat16))
    stacked = jnp.stack(results, axis=1)
    return stacked.reshape(
        own_count, 2, offset_count, harmonic_degree_total, 2, harmonic_degree_total
    )


def shards(frames, projection, degree_range, offsets):
    frame_rows, lat_rows, lon_count = frames.shape
    resident_wavenumbers, colatitude_total, harmonic_degree_total = projection.shape
    tm_count = lax.axis_size("tm")
    latitude_groups = lax.axis_size("lat")
    frame_count = frame_rows * tm_count
    azimuthal_order_count = resident_wavenumbers * tm_count * latitude_groups
    slots = jnp.arange(azimuthal_order_count, dtype=jnp.int32)
    table = longitude_table(lon_count, slots)
    azimuthal = jnp.dot(
        frames.reshape(frame_rows * lat_rows, lon_count), table, preferred_element_type=jnp.float32
    )
    azimuthal = azimuthal.astype(jnp.bfloat16).reshape(
        frame_rows, lat_rows, 2 * azimuthal_order_count
    )
    moved = lax.all_to_all(azimuthal[None], ("tm", "lat"), split_axis=3, concat_axis=0, tiled=True)
    grid = moved.reshape(tm_count, latitude_groups, frame_rows, lat_rows, resident_wavenumbers, 2)
    bands = projection.reshape(
        resident_wavenumbers, latitude_groups, lat_rows, harmonic_degree_total
    )
    summed = jnp.einsum("ijtaop,ojal->opitl", grid, bands, preferred_element_type=jnp.float32)
    summed = summed.reshape(resident_wavenumbers, 2, frame_count, harmonic_degree_total)
    device_rank = lax.axis_index("tm") * latitude_groups + lax.axis_index("lat")
    bounds = lax.dynamic_slice_in_dim(
        degree_range, device_rank * resident_wavenumbers, resident_wavenumbers, 0
    )
    degrees = jnp.arange(harmonic_degree_total, dtype=jnp.int32)
    keep = ((degrees[None, :] >= bounds[:, 0:1]) & (degrees[None, :] < bounds[:, 1:2])).astype(
        jnp.float32
    )
    harmonic = (summed * keep[:, None, None, :]).astype(jnp.bfloat16)
    harmonic = harmonic.reshape(resident_wavenumbers, 2 * frame_count, harmonic_degree_total)
    transform = time_table(frame_count)
    spectrum = jnp.einsum(
        "wr,orl->owl", transform, harmonic, preferred_element_type=jnp.float32
    ).astype(jnp.bfloat16)
    following = shifted_2(spectrum, ("tm", "lat"), -1)
    combined = jnp.concatenate([spectrum, following], axis=0)
    partners = jnp.stack(
        [combined[1 : resident_wavenumbers + 1], combined[2 : resident_wavenumbers + 2]], axis=1
    )
    return couple(spectrum, partners, offsets, frame_count)


def solution(mesh):
    return jax.shard_map(
        shards,
        mesh=mesh,
        in_specs=(P("tm", "lat", None), P(("tm", "lat"), None, None), P(), P()),
        out_specs=P(("tm", "lat"), None, None, None, None, None),
        check_vma=False,
    )
```

profile of v0, /device:TPU:0, one launch (start us, length us, event | category | flops | bytes accessed | tf_op | source)
XLA Modules:
  0.0 117.7 jit_solution(6313434164657998945)
XLA Ops:
  0.0 0.0 copy-start
  0.0 4.4 %multiply_convert_fusion.2 = (bf16[1024,256,1]{1,0,2:T(8,128)(2,1)S(1)}, bf16[1024,256,1]{1,0,2:T(8,128)(2,1)S(1)}) fusion(), kind=kLoop, calls=%fused_computation.28 | loop fusion | flops 4980736 | bytes 1048576 | tf_op jit(solution)/shard_map/convert.7
  4.4 0.1 pad_maximum_fusion.1
  4.5 2.1 %copy.49 = bf16[1024,256,2]{0,2,1:T(2,128)(2,1)} copy(bf16[1024,256,2]{1,0,2:T(8,128)(2,1)S(1)} %pad_maximum_fusion.1) | data formatting | bytes 2097152 | tf_op jit(solution)/shard_map/stack | solution.py:20
  6.6 1.5 %convert_element_type.73 = bf16[1024,512]{0,1:T(8,128)(2,1)S(1)} reshape(bf16[1024,256,2]{0,2,1:T(2,128)(2,1)} %copy.49) | data formatting | bytes 2097152 | tf_op jit(solution)/shard_map/convert_element_type | solution.py:21
  8.1 0.0 copy-done
  8.1 2.3 %fusion.4 = bf16[1024,512]{0,1:T(8,128)(2,1)} fusion(bf16[1024,512]{0,1:T(8,128)(2,1)S(1)} %convert_element_type.73, bf16[1024,1024]{1,0:T(8,128)(2,1)S(1)} %bitcast.79), kind=kOutput, calls=%fused_computation.13 | convolution fusion | flops 1074266112 | bytes 4194304 | tf_op jit(solution)/shard_map/dot_general | solution.py:73
  10.4 1.5 %copy.50 = bf16[1024,512]{1,0:T(8,128)(2,1)S(1)} copy(bf16[1024,512]{0,1:T(8,128)(2,1)} %fusion.4) | data formatting | bytes 2097152 | tf_op jit(solution)/shard_map/convert_element_type | solution.py:76
  11.9 6.4 %copy.51 = bf16[1,32,32,512]{2,1,0,3:T(8,128)(2,1)} copy(bf16[1,32,32,512]{3,2,1,0:T(8,128)(2,1)S(1)} %bitcast.86) | data formatting | bytes 2097152 | tf_op jit(solution)/shard_map/broadcast_in_dim;reshape | solution.py:79
  18.3 0.0 copy-start.2
  18.3 7.3 %reshape.204 = bf16[128,2,2048]{2,1,0:T(2,128)(2,1)} reshape(bf16[512,1,32,32]{3,2,1,0:T(8,128)(2,1)} %bitcast.80) | data formatting | bytes 2097152
  25.6 11.2 %all-to-all-start = ((bf16[128,2,2048]{2,1,0:T(2,128)(2,1)}), bf16[128,2,2048]{2,1,0:T(2,128)(2,1)S(1)}, u32[]{:S(2)}, u32[]{:S(2)}) async-start(bf16[128,2,2048]{2,1,0:T(2,128)(2,1)} %reshape.204), calls=%async_computation | async-start | bytes 2097152 | tf_op jit(solution)/shard_map/all_to_all | solution.py:79
  36.8 0.0 copy-done.2
  36.8 0.1 constant_dynamic-slice_fusion
  36.9 1.0 fusion.32
  37.9 1.1 negate_convert_fusion
  39.0 0.1 and_convert_fusion
  39.1 16.7 %all-to-all-done = bf16[128,2,2048]{2,1,0:T(2,128)(2,1)S(1)} async-done(((bf16[128,2,2048]{2,1,0:T(2,128)(2,1)}), bf16[128,2,2048]{2,1,0:T(2,128)(2,1)S(1)}, u32[]{:S(2)}, u32[]{:S(2)}) %all-to-all-start) | async-done | bytes 1048608 | tf_op jit(solution)/shard_map/all_to_all | solution.py:79
  55.8 3.5 %reshape.205 = bf16[512,1,32,32]{3,2,1,0:T(8,128)(2,1)} reshape(bf16[128,2,2048]{2,1,0:T(2,128)(2,1)S(1)} %all-to-all-done) | data formatting | bytes 2097152
  59.3 3.2 %fusion.5 = f32[2,2,8,32,256]{4,3,1,2,0:T(8,128)S(1)} fusion(bf16[2,16,32,256,1,1]{3,2,1,5,4,0:T(8,128)(2,1)} %bitcast.90, bf16[8,16,32,32,2,2]{3,2,5,4,1,0:T(8,128)(2,1)} %bitcast.85), kind=kOutput, calls=%fused_computation.14 | convolution fusion | flops 268435456 | bytes 2621440 | tf_op jit(solution)/shard_map/ijtaop,ojal->opitl/dot_general | solution.py:84
  62.5 0.0 copy-start.1
  62.5 0.1 copy.53
  62.6 0.1 fusion.12
  62.7 0.5 fusion.8
  63.2 1.5 %collective-permute-start = (bf16[2,512,256]{1,2,0:T(8,128)(2,1)S(1)}, bf16[2,512,256]{1,2,0:T(8,128)(2,1)S(1)}, u32[]{:S(2)}, u32[]{:S(2)}) collective-permute-start(bf16[2,512,256]{1,2,0:T(8,128)(2,1)S(1)} %fusion.8), channel_id=1, source_target_pairs={{1,0},{2,1},{3,2},{4,3},{5,4},{6,5},{7,6},{8,7},{9,8},{10,9},{11,1... | collective-permute-start | bytes 1572872 | tf_op jit(solution)/shard_map/ppermute | solution.py:12
  64.6 0.0 copy-done.1
  64.6 0.1 add_select_fusion.2
  64.7 1.0 copy.72
  65.7 2.6 %convert_bitcast_fusion = bf16[2,8,2,256,256]{4,3,1,2,0:T(8,128)(2,1)S(1)} fusion(bf16[2,2,256,256,1]{3,2,4,1,0:T(8,128)(2,1)} %bitcast.89, s32[8,256]{1,0:T(8,128)S(1)} %add_select_fusion.2), kind=kOutput, calls=%fused_computation.5 | convolution fusion | flops 1076363264 | bytes 4726784 | tf_op jit(solution)/shard_map/kwv,oqvl->okqwl/dot_general | solution.py:43
  68.3 0.4 copy.56
  68.7 9.4 %collective-permute-done = bf16[2,512,256]{1,2,0:T(8,128)(2,1)S(1)} collective-permute-done((bf16[2,512,256]{1,2,0:T(8,128)(2,1)S(1)}, bf16[2,512,256]{1,2,0:T(8,128)(2,1)S(1)}, u32[]{:S(2)}, u32[]{:S(2)}) %collective-permute-start) | collective-permute-done | bytes 524320 | tf_op jit(solution)/shard_map/ppermute | solution.py:12
  78.2 0.1 fusion.17
  78.3 0.1 maximum_maximum_fusion
  78.5 5.2 %multiply_convert_fusion = bf16[2,8,256,512]{3,2,1,0:T(8,128)(2,1)} fusion(bf16[2,8,512,256]{3,2,1,0:T(8,128)(2,1)S(1)} %bitcast.87, bf16[2,2,512,512]{2,3,0,1:T(8,128)(2,1)S(1)} %maximum_maximum_fusion), kind=kOutput, calls=%fused_computation.1 | convolution fusion | flops 2151677952 | bytes 9437184 | tf_op jit(solution)/shard_map/okrl,orm->oklm/dot_general | solution.py:54
  83.6 5.1 %multiply_convert_fusion.1 = bf16[2,8,256,512]{3,2,1,0:T(8,128)(2,1)} fusion(bf16[2,8,512,256]{3,2,1,0:T(8,128)(2,1)S(1)} %bitcast.88, bf16[2,2,512,512]{2,3,0,1:T(8,128)(2,1)S(1)} %maximum_maximum_fusion), kind=kOutput, calls=%fused_computation.2 | convolution fusion | flops 2151677952 | bytes 9437184 | tf_op jit(solution)/shard_map/okrl,orm->oklm/dot_general | solution.py:54
  88.8 6.9 %stack.28 = bf16[2,1,8,256,2,256]{5,4,3,2,0,1:T(2,128)(2,1)} reshape(bf16[2,8,256,512]{3,2,1,0:T(8,128)(2,1)} %multiply_convert_fusion.1) | data formatting | bytes 8388608 | tf_op jit(solution)/shard_map/stack | solution.py:58
  95.7 7.0 %stack.29 = bf16[2,1,8,256,2,256]{5,4,3,2,0,1:T(2,128)(2,1)} reshape(bf16[2,8,256,512]{3,2,1,0:T(8,128)(2,1)} %multiply_convert_fusion) | data formatting | bytes 8388608 | tf_op jit(solution)/shard_map/stack | solution.py:58
  102.7 14.8 %pad_maximum_fusion = bf16[2,2,8,256,2,256]{5,4,3,2,1,0:T(2,128)(2,1)} fusion(bf16[2,1,8,256,2,256]{5,4,3,2,1,0:T(2,128)(2,1)} %bitcast.82, bf16[2,1,8,256,2,256]{5,4,3,2,1,0:T(2,128)(2,1)} %bitcast.81), kind=kLoop, calls=%fused_computation | loop fusion | flops 4194304 | bytes 16777216 | tf_op jit(solution)/shard_map/stack | solution.py:58
  (2 shorter events, 0.1 us)
Async XLA Ops:
  0.0 8.1 %copy-start = (bf16[32,32,1024]{2,1,0:T(8,128)(2,1)S(1)}, bf16[32,32,1024]{2,1,0:T(8,128)(2,1)}, u32[]{:S(2)}) copy-start(bf16[32,32,1024]{2,1,0:T(8,128)(2,1)} %param.4) | copy-start | bytes 6291460
  18.3 18.5 %copy-start.2 = (s32[256,2]{0,1:T(2,128)S(1)}, s32[256,2]{0,1:T(2,128)}, u32[]{:S(2)}) copy-start(s32[256,2]{0,1:T(2,128)} %param.6) | copy-start | bytes 6148
  25.6 30.2 %all-to-all-start = ((bf16[128,2,2048]{2,1,0:T(2,128)(2,1)}), bf16[128,2,2048]{2,1,0:T(2,128)(2,1)S(1)}, u32[]{:S(2)}, u32[]{:S(2)}) async-start(bf16[128,2,2048]{2,1,0:T(2,128)(2,1)} %reshape.204), calls=%async_computation | async-start | bytes 2097152 | tf_op jit(solution)/shard_map/all_to_all | solution.py:79
  62.5 2.2 %copy-start.1 = (s32[8]{0:T(128)S(1)}, s32[8]{0:T(128)}, u32[]{:S(2)}) copy-start(s32[8]{0:T(128)} %param.7) | copy-start | bytes 100
  63.2 15.0 %collective-permute-start = (bf16[2,512,256]{1,2,0:T(8,128)(2,1)S(1)}, bf16[2,512,256]{1,2,0:T(8,128)(2,1)S(1)}, u32[]{:S(2)}, u32[]{:S(2)}) collective-permute-start(bf16[2,512,256]{1,2,0:T(8,128)(2,1)S(1)} %fusion.8), channel_id=1, source_target_pairs={{1,0},{2,1},{3,2},{4,3},{5,4},{6,5},{7,6},{8,7},{9,8},{10,9},{11,1... | collective-permute-start | bytes 1572872 | tf_op jit(solution)/shard_map/ppermute | solution.py:12
where the time goes:
time: 119 us; the launch traced here: 118 us
  local copies, waits for them, and re-layouts  37.7 us (32%)
  waiting for transfers between devices  26.1 us (22%)
  other arithmetic  22 us (18%)
  matrix products  18.8 us (16%)
  starting transfers between devices  12.6 us (11%)
    all_to_all x1, waiting for transfers between devices, shards(): lax.all_to_all(azimuthal[None], ('tm', 'lat'), split_axis=3, concat_axis=...  16.7 us
    another operation x1, other arithmetic, couple(): stacked = jnp.stack(results, axis=1)  14.8 us
    another operation x2, local copies, waits for them, and re-layouts, couple(): stacked = jnp.stack(results, axis=1)  13.9 us
    all_to_all x1, starting transfers between devices, shards(): lax.all_to_all(azimuthal[None], ('tm', 'lat'), split_axis=3, concat_axis=...  11.2 us
    unnamed x8, local copies, waits for them, and re-layouts  10.8 us
    dot_general x2, matrix products, couple(): jnp.einsum('okrl,orm->oklm', shifted, both[:, partner_index], preferred_e...  10.3 us
    ppermute x1, waiting for transfers between devices, shifted_2(): return lax.ppermute(block, axis, route)  9.38 us
    another operation x3, other arithmetic  6.5 us
  transfers between devices with their start and end apart: 2, of which 2 were waited for; matrix products, arithmetic and copies ran while one was open for 5% of the time, Pallas kernels for 0%

commit v1 on v0

v1 whole, which is shorter than its diff:
```python
import math

import jax
import jax.numpy as jnp
import numpy as np
from jax import lax
from jax.experimental import pallas as pl
from jax.experimental.pallas import tpu as pltpu
from jax.sharding import PartitionSpec as P

BF = jnp.bfloat16
F32 = jnp.float32


def longitude_table(lon_count, orders):
    pairs = orders // 2
    gh, op, gl = np.meshgrid(
        np.arange(pairs // 32), np.arange(4), np.arange(32), indexing="ij"
    )
    order = (2 * (32 * gh + gl) + op // 2).reshape(-1)
    part = (op % 2).reshape(-1)
    phase = np.arange(lon_count)[:, None] * order[None, :] % lon_count
    angle = phase * (2.0 * math.pi / lon_count)
    table = np.where(part[None, :] == 0, np.cos(angle), -np.sin(angle))
    return jnp.asarray((table / math.sqrt(lon_count)).astype(np.float32)).astype(BF)


def swap_index_and_lanes(values, unit):
    values = list(values)
    lane = lax.broadcasted_iota(jnp.int32, values[0].shape, 1)
    step = len(values) // 2
    while step:
        low = (lane & (step * unit)) == 0
        for i in range(len(values)):
            if i & step == 0:
                a, b = values[i], values[i + step]
                values[i] = jnp.where(low, a, pltpu.roll(b, step * unit, 1))
                values[i + step] = jnp.where(
                    low, pltpu.roll(a, 128 - step * unit, 1), b
                )
        step //= 2
    return values


def longitude_kernel(x_ref, table_ref, s_ref):
    for bh in range(2):
        rows = slice(16 * bh, 16 * bh + 16)
        lhs = x_ref[:, rows, :].reshape(512, 1024)
        for gp in range(2):
            z = jnp.dot(
                lhs, table_ref[:, 256 * gp : 256 * gp + 256], preferred_element_type=F32
            )
            z = z.astype(BF).reshape(32, 16, 256)
            for c in range(2):
                v = [z[t, :, 128 * c : 128 * c + 128] for t in range(32)]
                v = swap_index_and_lanes(v, 1)
                for gl in range(32):
                    s_ref[32 * (2 * gp + c) + gl, rows, :] = v[gl]


def latitude_kernel(range_ref, r_ref, proj_ref, h_ref, a_ref):
    @pl.loop(0, 32)
    def _(i):
        rows = pl.ds(pl.multiple_of(i * 16, 16), 16)
        for q in range(2):
            v = [r_ref[4 * q + j, rows, :] for j in range(4)]
            v = swap_index_and_lanes(v, 32)
            for op in range(4):
                lanes = slice(256 * (op % 2) + 128 * q, 256 * (op % 2) + 128 * q + 128)
                a_ref[op // 2, rows, lanes] = v[op]

    device = lax.axis_index("tm") * lax.axis_size("lat") + lax.axis_index("lat")
    degree = lax.broadcasted_iota(jnp.int32, (256, 512), 0)
    for o in range(2):
        h = lax.dot_general(
            proj_ref[o], a_ref[o], (((0,), (0,)), ((), ())), preferred_element_type=F32
        )
        low, high = range_ref[2 * device + o, 0], range_ref[2 * device + o, 1]
        keep = (degree >= low) & (degree < high)
        h_ref[o] = jnp.where(keep, h, 0.0).astype(BF)


def coupling_kernel(own_ref, next_ref, cos_ref, sin_ref, out_ref, twice_ref, partner_ref):
    o, k = pl.program_id(0), pl.program_id(1)

    @pl.when((o == 0) & (k == 0))
    def _():
        partner_ref[0] = own_ref[1]
        partner_ref[1] = next_ref[0]
        partner_ref[2] = next_ref[1]

    @pl.when(k == 0)
    def _():
        row = lax.broadcasted_iota(jnp.int32, (512, 256), 0)
        column = lax.broadcasted_iota(jnp.int32, (512, 256), 1)
        double = ((row >> 1) == column).astype(F32).astype(BF)
        twice_ref[...] = jnp.dot(double, own_ref[o], preferred_element_type=F32)

    cos = jnp.broadcast_to(cos_ref[k][None], (64, 8, 256)).reshape(512, 256)
    sin = jnp.broadcast_to(sin_ref[k][None], (64, 8, 256)).reshape(512, 256)
    real, imag = twice_ref[:, :256], twice_ref[:, 256:]
    left = jnp.concatenate(
        [
            (real * cos - imag * sin).astype(BF),
            (real * sin + imag * cos).astype(BF),
        ],
        axis=1,
    )
    for s in range(2):
        product = lax.dot_general(
            left,
            partner_ref[o + s],
            (((1,), (1,)), ((), ())),
            preferred_element_type=F32,
        )
        out_ref[0, s, 0] = product.astype(BF).reshape(256, 2, 256)


def whole(shape):
    return pl.BlockSpec(shape, lambda *_: (0,) * len(shape))


def phase_tables(offsets, frame_count):
    t = jnp.arange(frame_count, dtype=jnp.int32)
    turn = (offsets[:, None] * t[None, :]) % frame_count
    angle = turn.astype(F32) * (2.0 * math.pi / frame_count)
    scale = 1.0 / math.sqrt(frame_count)
    cos, sin = jnp.cos(angle) * scale, jnp.sin(angle) * scale
    odd = (jnp.arange(8) % 2 == 1)[None, :, None]
    return (
        jnp.where(odd, -sin[:, None], cos[:, None]),
        jnp.where(odd, cos[:, None], sin[:, None]),
    )


def shards(frames, projection, degree_range, offsets):
    table = longitude_table(1024, 256)
    sent = pl.pallas_call(
        longitude_kernel,
        out_shape=jax.ShapeDtypeStruct((128, 32, 128), BF),
        cost_estimate=pl.CostEstimate(
            flops=2**30, bytes_accessed=4 << 20, transcendentals=0
        ),
        name="longitude",
    )(frames, table)
    got = lax.all_to_all(sent, ("tm", "lat"), split_axis=0, concat_axis=0, tiled=True)
    harmonic = pl.pallas_call(
        latitude_kernel,
        in_specs=[
            pl.BlockSpec(memory_space=pltpu.SMEM),
            pl.BlockSpec(memory_space=pltpu.VMEM),
            pl.BlockSpec(memory_space=pltpu.VMEM),
        ],
        out_shape=jax.ShapeDtypeStruct((2, 256, 512), BF),
        scratch_shapes=[pltpu.VMEM((2, 512, 512), BF)],
        cost_estimate=pl.CostEstimate(
            flops=2**28, bytes_accessed=2 << 20, transcendentals=0
        ),
        name="latitude",
    )(degree_range, got.reshape(8, 512, 128), projection)
    devices = range(128)
    following = lax.ppermute(
        harmonic, ("tm", "lat"), [(i, i - 1) for i in devices if i > 0]
    )
    cos, sin = phase_tables(offsets, 256)
    return pl.pallas_call(
        coupling_kernel,
        grid=(2, 8),
        in_specs=[
            whole((2, 256, 512)),
            whole((2, 256, 512)),
            whole((8, 8, 256)),
            whole((8, 8, 256)),
        ],
        out_specs=pl.BlockSpec(
            (1, 2, 1, 256, 2, 256), lambda o, k: (o, 0, k, 0, 0, 0)
        ),
        out_shape=jax.ShapeDtypeStruct((2, 2, 8, 256, 2, 256), BF),
        scratch_shapes=[
            pltpu.VMEM((512, 512), F32),
            pltpu.VMEM((3, 256, 512), BF),
        ],
        cost_estimate=pl.CostEstimate(
            flops=2**32, bytes_accessed=10 << 20, transcendentals=0
        ),
        name="coupling",
    )(harmonic, following, cos, sin)


def solution(mesh):
    return jax.shard_map(
        shards,
        mesh=mesh,
        in_specs=(P("tm", "lat", None), P(("tm", "lat"), None, None), P(), P()),
        out_specs=P(("tm", "lat"), None, None, None, None, None),
        check_vma=False,
    )
```

time: 119 us -> 74.9 us (0.63)
  local copies, waits for them, and re-layouts: 37.7 us -> 3.22 us
  Pallas kernels: 0 us -> 26.6 us
  other arithmetic: 22 us -> 0.87 us
  matrix products: 18.8 us -> 0 us
  waiting for transfers between devices: 26.1 us -> 30.6 us
    pallas_call x0 -> x3, Pallas kernels: none -> 26.6 us  [the longest x1 12.8 us: shards(): pl.pallas_call(coupling_kernel, grid=(2, 8), in_specs=[whole((2, 256, 512...]
    another operation x4 -> x0, local copies, waits for them, and re-layouts: 22.4 us -> none  [the longest x2 13.9 us: couple(): stacked = jnp.stack(results, axis=1)]
    another operation x7 -> x0, other arithmetic: 21.6 us -> none  [the longest x1 14.8 us: couple(): stacked = jnp.stack(results, axis=1)]
    dot_general x6 -> x0, matrix products: 18.8 us -> none  [the longest x2 10.3 us: couple(): jnp.einsum('okrl,orm->oklm', shifted, both[:, partner_index], preferred_e...]
    unnamed x8 -> x7, local copies, waits for them, and re-layouts: 10.8 us -> 3.22 us
    ppermute x1, waiting for transfers between devices: 9.38 us -> 13 us  [shards(): lax.ppermute(harmonic, ('tm', 'lat'), [(i, i - 1) for i in devices if i >...]
    convert_element_type x3 -> x0, local copies, waits for them, and re-layouts: 3.39 us -> none  [the longest x1 1.49 us: shards(): azimuthal.astype(jnp.bfloat16)]
  transfers between devices with their start and end apart: 2 -> 2, of which waited for: 2 -> 2; matrix products, arithmetic and copies ran while one was open for 5% -> 3% of each run, Pallas kernels for 0% -> 0%
where the time goes in v1:
time: 74.9 us; the launch traced here: 73.8 us
  waiting for transfers between devices  30.6 us (41%)
  Pallas kernels  26.6 us (36%)
  starting transfers between devices  12.5 us (17%)
  local copies, waits for them, and re-layouts  3.22 us (4%)
  other arithmetic  0.87 us (1%)
    all_to_all x1, waiting for transfers between devices, shards(): lax.all_to_all(sent, ('tm', 'lat'), split_axis=0, concat_axis=0, tiled=True)  17.6 us
    ppermute x1, waiting for transfers between devices, shards(): lax.ppermute(harmonic, ('tm', 'lat'), [(i, i - 1) for i in devices if i >...  13 us
    pallas_call x1, Pallas kernels, shards(): pl.pallas_call(coupling_kernel, grid=(2, 8), in_specs=[whole((2, 256, 512...  12.8 us
    all_to_all x1, starting transfers between devices, shards(): lax.all_to_all(sent, ('tm', 'lat'), split_axis=0, concat_axis=0, tiled=True)  11.2 us
    pallas_call x1, Pallas kernels, shards(): pl.pallas_call(latitude_kernel, in_specs=[pl.BlockSpec(memory_space=pltpu...  8.88 us
    pallas_call x1, Pallas kernels, shards(): pl.pallas_call(longitude_kernel, out_shape=jax.ShapeDtypeStruct((128, 32,...  4.95 us
    unnamed x7, local copies, waits for them, and re-layouts  3.22 us
  transfers between devices with their start and end apart: 2, of which 2 were waited for; matrix products, arithmetic and copies ran while one was open for 3% of the time, Pallas kernels for 0%

profile of v1, /device:TPU:0, one launch (start us, length us, event | category | flops | bytes accessed | tf_op | source)
XLA Modules:
  0.0 73.8 jit_solution(2991190852349334304)
XLA Ops:
  0.0 0.0 copy-start.1
  0.0 5.0 %longitude.1 = bf16[128,32,128]{2,1,0:T(8,128)(2,1)} custom-call(bf16[32,32,1024]{2,1,0:T(8,128)(2,1)} %x_ref.1, bf16[1024,512]{1,0:T(8,128)(2,1)} %constant.39.table_ref), custom_call_target="tpu_custom_call" | custom-call | flops 1073741824 | bytes 4194304 | tf_op jit(solution)/shard_map/longitude/pallas_call | solution.py:138
  5.0 11.2 %all-to-all-start = ((bf16[128,32,128]{2,1,0:T(8,128)(2,1)}), bf16[128,32,128]{2,1,0:T(8,128)(2,1)S(1)}, u32[]{:S(2)}, u32[]{:S(2)}) async-start(bf16[128,32,128]{2,1,0:T(8,128)(2,1)} %longitude.1), calls=%async_computation | async-start | bytes 2097152 | tf_op jit(solution)/shard_map/all_to_all | solution.py:146
  16.1 1.5 %copy.6.range_ref = s32[256,2]{1,0:T(8,128)} copy(s32[256,2]{0,1:T(2,128)} %param.7) | data formatting | bytes 4096 | tf_op args[2]
  17.6 17.6 %all-to-all-done = bf16[128,32,128]{2,1,0:T(8,128)(2,1)S(1)} async-done(((bf16[128,32,128]{2,1,0:T(8,128)(2,1)}), bf16[128,32,128]{2,1,0:T(8,128)(2,1)S(1)}, u32[]{:S(2)}, u32[]{:S(2)}) %all-to-all-start) | async-done | bytes 1048608 | tf_op jit(solution)/shard_map/all_to_all | solution.py:146
  35.2 0.0 copy-start
  35.2 1.0 %copy-done = bf16[128,32,128]{2,1,0:T(8,128)(2,1)} copy-done((bf16[128,32,128]{2,1,0:T(8,128)(2,1)}, bf16[128,32,128]{2,1,0:T(8,128)(2,1)S(1)}, u32[]{:S(2)}) %copy-start) | copy-done | bytes 1048600
  36.1 8.9 %latitude.1.own_ref = bf16[2,256,512]{2,1,0:T(8,128)(2,1)} custom-call(s32[256,2]{1,0:T(8,128)} %copy.6.range_ref, bf16[8,512,128]{2,1,0:T(8,128)(2,1)} %bitcast.1, bf16[2,512,256]{2,1,0:T(8,128)(2,1)} %proj_ref.1), custom_call_target="tpu_custom_call" | custom-call | flops 268435456 | bytes 2097152 | tf_op jit(solution)/shard_map/latitude/pallas_call | solution.py:147
  45.0 1.3 %collective-permute-start = (bf16[2,256,512]{2,1,0:T(8,128)(2,1)}, bf16[2,256,512]{2,1,0:T(8,128)(2,1)S(1)}, u32[]{:S(2)}, u32[]{:S(2)}) collective-permute-start(bf16[2,256,512]{2,1,0:T(8,128)(2,1)} %latitude.1.own_ref), channel_id=1, source_target_pairs={{1,0},{2,1},{3,2},{4,3},{5,4},{6,5},{7,6},{8,7},{9,8},{10,9},{11,1... | collective-permute-start | bytes 1572872 | tf_op jit(solution)/shard_map/ppermute | solution.py:162
  46.3 0.0 copy-done.1
  46.3 0.1 sine_multiply_fusion
  46.5 0.7 broadcast_select_fusion
  47.2 13.0 %collective-permute-done.next_ref = bf16[2,256,512]{2,1,0:T(8,128)(2,1)S(1)} collective-permute-done((bf16[2,256,512]{2,1,0:T(8,128)(2,1)}, bf16[2,256,512]{2,1,0:T(8,128)(2,1)S(1)}, u32[]{:S(2)}, u32[]{:S(2)}) %collective-permute-start) | collective-permute-done | bytes 524320 | tf_op jit(solution)/shard_map/ppermute | solution.py:162
  60.2 0.0 copy-start.2
  60.2 0.8 %copy-done.2 = bf16[2,256,512]{2,1,0:T(8,128)(2,1)} copy-done((bf16[2,256,512]{2,1,0:T(8,128)(2,1)}, bf16[2,256,512]{2,1,0:T(8,128)(2,1)S(1)}, u32[]{:S(2)}) %copy-start.2) | copy-done | bytes 524312
  61.0 12.8 %coupling.1 = bf16[2,2,8,256,2,256]{5,4,3,2,1,0:T(2,128)(2,1)} custom-call(bf16[2,256,512]{2,1,0:T(8,128)(2,1)} %latitude.1.own_ref, bf16[2,256,512]{2,1,0:T(8,128)(2,1)} %copy-done.2, f32[8,8,256]{2,1,0:T(8,128)} %get-tuple-element.6.cos_ref, f32[8,8,256]{2,1,0:T(8,128)} %get-tuple-element.5.sin_ref), custom_call_target="tpu_custom_call" | custom-call | flops 4294967296 | bytes 10485760 | tf_op jit(solution)/shard_map/coupling/pallas_call | solution.py:166
  (1 shorter events, 0.0 us)
Async XLA Ops:
  0.0 46.3 %copy-start.1 = (s32[8]{0:T(128)S(1)}, s32[8]{0:T(128)}, u32[]{:S(2)}) copy-start(s32[8]{0:T(128)} %param.8) | copy-start | bytes 100
  5.0 30.2 %all-to-all-start = ((bf16[128,32,128]{2,1,0:T(8,128)(2,1)}), bf16[128,32,128]{2,1,0:T(8,128)(2,1)S(1)}, u32[]{:S(2)}, u32[]{:S(2)}) async-start(bf16[128,32,128]{2,1,0:T(8,128)(2,1)} %longitude.1), calls=%async_computation | async-start | bytes 2097152 | tf_op jit(solution)/shard_map/all_to_all | solution.py:146
  35.2 1.0 %copy-start = (bf16[128,32,128]{2,1,0:T(8,128)(2,1)}, bf16[128,32,128]{2,1,0:T(8,128)(2,1)S(1)}, u32[]{:S(2)}) copy-start(bf16[128,32,128]{2,1,0:T(8,128)(2,1)S(1)} %all-to-all-done) | copy-start | bytes 3145732
  45.0 15.2 %collective-permute-start = (bf16[2,256,512]{2,1,0:T(8,128)(2,1)}, bf16[2,256,512]{2,1,0:T(8,128)(2,1)S(1)}, u32[]{:S(2)}, u32[]{:S(2)}) collective-permute-start(bf16[2,256,512]{2,1,0:T(8,128)(2,1)} %latitude.1.own_ref), channel_id=1, source_target_pairs={{1,0},{2,1},{3,2},{4,3},{5,4},{6,5},{7,6},{8,7},{9,8},{10,9},{11,1... | collective-permute-start | bytes 1572872 | tf_op jit(solution)/shard_map/ppermute | solution.py:162
  60.2 0.8 %copy-start.2 = (bf16[2,256,512]{2,1,0:T(8,128)(2,1)}, bf16[2,256,512]{2,1,0:T(8,128)(2,1)S(1)}, u32[]{:S(2)}) copy-start(bf16[2,256,512]{2,1,0:T(8,128)(2,1)S(1)} %collective-permute-done.next_ref) | copy-start | bytes 1572868

commit v2 on v1

--- a/solution.py
+++ b/solution.py
@@ -12,12 +12,18 @@
 F32 = jnp.float32
 
 
-def longitude_table(lon_count, orders):
-    pairs = orders // 2
-    gh, op, gl = np.meshgrid(
-        np.arange(pairs // 32), np.arange(4), np.arange(32), indexing="ij"
-    )
-    order = (2 * (32 * gh + gl) + op // 2).reshape(-1)
+def destination(chunk, slot):
+    x, y, core = slot // 8, slot // 2 % 4, slot % 2
+    z = (chunk + 8 - x - y) % 4
+    return 2 * z + core, 4 * x + y
+
+
+def longitude_table(lon_count):
+    chunk, op, slot = np.meshgrid(
+        np.arange(4), np.arange(4), np.arange(32), indexing="ij"
+    )
+    tm, lat = destination(chunk, slot)
+    order = (2 * (16 * tm + lat) + op // 2).reshape(-1)
     part = (op % 2).reshape(-1)
     phase = np.arange(lon_count)[:, None] * order[None, :] % lon_count
     angle = phase * (2.0 * math.pi / lon_count)
@@ -42,42 +48,82 @@
     return values
 
 
-def longitude_kernel(x_ref, table_ref, s_ref):
-    for bh in range(2):
-        rows = slice(16 * bh, 16 * bh + 16)
-        lhs = x_ref[:, rows, :].reshape(512, 1024)
-        for gp in range(2):
+def transform_kernel(
+    range_ref, x_ref, table_ref, proj_ref, h_ref, s_ref, r_ref, a_ref, send_sem, recv_sem
+):
+    tm, lat = lax.axis_index("tm"), lax.axis_index("lat")
+    me = 16 * tm + lat
+    barrier = pltpu.get_barrier_semaphore()
+
+    @pl.loop(1, 128)
+    def _(i):
+        peer = (me + i) % 128
+        pl.semaphore_signal(barrier, inc=1, device_id=(peer // 16, peer % 16))
+
+    for gp in range(2):
+        for bh in range(2):
+            rows = slice(16 * bh, 16 * bh + 16)
             z = jnp.dot(
-                lhs, table_ref[:, 256 * gp : 256 * gp + 256], preferred_element_type=F32
+                x_ref[:, rows, :].reshape(512, 1024),
+                table_ref[:, 256 * gp : 256 * gp + 256],
+                preferred_element_type=F32,
             )
             z = z.astype(BF).reshape(32, 16, 256)
             for c in range(2):
                 v = [z[t, :, 128 * c : 128 * c + 128] for t in range(32)]
                 v = swap_index_and_lanes(v, 1)
-                for gl in range(32):
-                    s_ref[32 * (2 * gp + c) + gl, rows, :] = v[gl]
-
-
-def latitude_kernel(range_ref, r_ref, proj_ref, h_ref, a_ref):
-    @pl.loop(0, 32)
-    def _(i):
-        rows = pl.ds(pl.multiple_of(i * 16, 16), 16)
+                for slot in range(32):
+                    s_ref[32 * (2 * gp + c) + slot, rows, :] = v[slot]
+        if gp == 0:
+            pl.semaphore_wait(barrier, 127)
+
+        @pl.loop(0, 64)
+        def _(i):
+            chunk, slot = 2 * gp + i % 2, (i // 2 + 2 * lat + tm) % 32
+            to_tm, to_lat = destination(chunk, slot)
+
+            @pl.when((to_tm != tm) | (to_lat != lat))
+            def _():
+                pltpu.make_async_remote_copy(
+                    src_ref=s_ref.at[32 * chunk + slot],
+                    dst_ref=r_ref.at[me],
+                    send_sem=send_sem,
+                    recv_sem=recv_sem,
+                    device_id=(to_tm, to_lat),
+                ).start()
+
+    x, y = lat // 4, lat % 4
+    mine = 32 * ((x + y + tm // 2) % 4) + 8 * x + 2 * y + tm % 2
+    r_ref[me] = s_ref[mine]
+    rest = pltpu.make_async_remote_copy(
+        src_ref=s_ref.at[pl.ds(0, 127)],
+        dst_ref=r_ref.at[pl.ds(0, 127)],
+        send_sem=send_sem,
+        recv_sem=recv_sem,
+        device_id=(tm, lat),
+    )
+    rest.wait_recv()
+
+    for i in range(32):
+        rows = slice(16 * i, 16 * i + 16)
         for q in range(2):
-            v = [r_ref[4 * q + j, rows, :] for j in range(4)]
+            v = [
+                r_ref[16 * (4 * q + j) + i // 2, 16 * (i % 2) : 16 * (i % 2) + 16, :]
+                for j in range(4)
+            ]
             v = swap_index_and_lanes(v, 32)
             for op in range(4):
-                lanes = slice(256 * (op % 2) + 128 * q, 256 * (op % 2) + 128 * q + 128)
-                a_ref[op // 2, rows, lanes] = v[op]
-
-    device = lax.axis_index("tm") * lax.axis_size("lat") + lax.axis_index("lat")
+                start = 256 * (op % 2) + 128 * q
+                a_ref[op // 2, rows, start : start + 128] = v[op]
     degree = lax.broadcasted_iota(jnp.int32, (256, 512), 0)
     for o in range(2):
         h = lax.dot_general(
             proj_ref[o], a_ref[o], (((0,), (0,)), ((), ())), preferred_element_type=F32
         )
-        low, high = range_ref[2 * device + o, 0], range_ref[2 * device + o, 1]
+        low, high = range_ref[2 * me + o, 0], range_ref[2 * me + o, 1]
         keep = (degree >= low) & (degree < high)
         h_ref[o] = jnp.where(keep, h, 0.0).astype(BF)
+    rest.wait_send()
 
 
 def coupling_kernel(own_ref, next_ref, cos_ref, sin_ref, out_ref, twice_ref, partner_ref):
@@ -134,30 +180,24 @@
 
 
 def shards(frames, projection, degree_range, offsets):
-    table = longitude_table(1024, 256)
-    sent = pl.pallas_call(
-        longitude_kernel,
-        out_shape=jax.ShapeDtypeStruct((128, 32, 128), BF),
+    harmonic = pl.pallas_call(
+        transform_kernel,
+        in_specs=[pl.BlockSpec(memory_space=pltpu.SMEM)]
+        + [pl.BlockSpec(memory_space=pltpu.VMEM)] * 3,
+        out_shape=jax.ShapeDtypeStruct((2, 256, 512), BF),
+        scratch_shapes=[
+            pltpu.VMEM((128, 32, 128), BF),
+            pltpu.VMEM((128, 32, 128), BF),
+            pltpu.VMEM((2, 512, 512), BF),
+            pltpu.SemaphoreType.DMA,
+            pltpu.SemaphoreType.DMA,
+        ],
+        compiler_params=pltpu.CompilerParams(collective_id=0, has_side_effects=True),
         cost_estimate=pl.CostEstimate(
             flops=2**30, bytes_accessed=4 << 20, transcendentals=0
         ),
-        name="longitude",
-    )(frames, table)
-    got = lax.all_to_all(sent, ("tm", "lat"), split_axis=0, concat_axis=0, tiled=True)
-    harmonic = pl.pallas_call(
-        latitude_kernel,
-        in_specs=[
-            pl.BlockSpec(memory_space=pltpu.SMEM),
-            pl.BlockSpec(memory_space=pltpu.VMEM),
-            pl.BlockSpec(memory_space=pltpu.VMEM),
-        ],
-        out_shape=jax.ShapeDtypeStruct((2, 256, 512), BF),
-        scratch_shapes=[pltpu.VMEM((2, 512, 512), BF)],
-        cost_estimate=pl.CostEstimate(
-            flops=2**28, bytes_accessed=2 << 20, transcendentals=0
-        ),
-        name="latitude",
-    )(degree_range, got.reshape(8, 512, 128), projection)
+        name="transform",
+    )(degree_range, frames, longitude_table(1024), projection)
     devices = range(128)
     following = lax.ppermute(
         harmonic, ("tm", "lat"), [(i, i - 1) for i in devices if i > 0]

time: 74.9 us -> 69.4 us (0.927)
  the two profiles are of different devices: /device:TPU:0 before, /device:TPU:24 now
where the time goes in v2:
time: 69.4 us; the launch traced here: 69.2 us
  Pallas kernels  49.1 us (71%)
  waiting for transfers between devices  14.3 us (21%)
  local copies, waits for them, and re-layouts  2.26 us (3%)
  starting transfers between devices  1.92 us (3%)
  other arithmetic  1.52 us (2%)
    pallas_call x1, Pallas kernels, shards(): pl.pallas_call(transform_kernel, in_specs=[pl.BlockSpec(memory_space=pltp...  36.4 us
    ppermute x1, waiting for transfers between devices, shards(): lax.ppermute(harmonic, ('tm', 'lat'), [(i, i - 1) for i in devices if i >...  14.3 us
    pallas_call x1, Pallas kernels, shards(): pl.pallas_call(coupling_kernel, grid=(2, 8), in_specs=[whole((2, 256, 512...  12.8 us
    unnamed x3, local copies, waits for them, and re-layouts  2.26 us
    ppermute x1, starting transfers between devices, shards(): lax.ppermute(harmonic, ('tm', 'lat'), [(i, i - 1) for i in devices if i >...  1.92 us
  transfers between devices with their start and end apart: 1, of which 1 were waited for; matrix products, arithmetic and copies ran while one was open for 2% of the time, Pallas kernels for 0%

profile of v2, /device:TPU:24, one launch (start us, length us, event | category | flops | bytes accessed | tf_op | source)
XLA Modules:
  0.0 69.2 jit_solution(14133982667824638962)
XLA Ops:
  0.0 1.5 %copy.6.range_ref = s32[256,2]{1,0:T(8,128)} copy(s32[256,2]{0,1:T(2,128)} %param.7) | data formatting | bytes 4096 | tf_op args[2]
  1.5 36.4 %transform.1.own_ref = bf16[2,256,512]{2,1,0:T(8,128)(2,1)} custom-call(s32[256,2]{1,0:T(8,128)} %copy.6.range_ref, bf16[32,32,1024]{2,1,0:T(8,128)(2,1)} %x_ref.1, bf16[1024,512]{1,0:T(8,128)(2,1)} %constant.39.table_ref, bf16[2,512,256]{2,1,0:T(8,128)(2,1)} %proj_ref.1), custom_call_target="tpu_custom_call" | custom-call | flops 1073741824 | bytes 4194304 | tf_op jit(solution)/shard_map/transform/pallas_call | solution.py:183
  37.8 1.9 %collective-permute-start = (bf16[2,256,512]{2,1,0:T(8,128)(2,1)}, bf16[2,256,512]{2,1,0:T(8,128)(2,1)S(1)}, u32[]{:S(2)}, u32[]{:S(2)}) collective-permute-start(bf16[2,256,512]{2,1,0:T(8,128)(2,1)} %transform.1.own_ref), channel_id=1, source_target_pairs={{1,0},{2,1},{3,2},{4,3},{5,4},{6,5},{7,6},{8,7},{9,8},{10,9},{11,1... | collective-permute-start | bytes 1572872 | tf_op jit(solution)/shard_map/ppermute | solution.py:202
  39.8 0.8 %sine_multiply_fusion = (f32[8,256]{1,0:T(8,128)S(1)}, f32[8,256]{1,0:T(8,128)S(1)}, f32[8,256]{1,0:T(8,128)S(1)}) fusion(s32[8]{0:T(128)} %param.8), kind=kLoop, calls=%fused_computation.9 | loop fusion | flops 34816 | bytes 24608 | tf_op jit(solution)/shard_map/mul | solution.py:174
  40.6 0.7 %broadcast_select_fusion = (f32[8,8,256]{2,1,0:T(8,128)}, f32[8,8,256]{2,1,0:T(8,128)}) fusion(f32[8,256]{1,0:T(8,128)S(1)} %get-tuple-element.7, f32[8,256]{1,0:T(8,128)S(1)} %get-tuple-element.9, pred[8]{0:T(512)(128)(4,1)S(1)} %fusion.7, f32[8,256]{1,0:T(8,128)S(1)} %get-tuple-element.8), kind=kLoop, calls=%fused_computation | loop fusion | flops 32768 | bytes 155656 | tf_op jit(solution)/shard_map/jit(_where)/select_n | solution.py:178
  41.3 14.3 %collective-permute-done.next_ref = bf16[2,256,512]{2,1,0:T(8,128)(2,1)S(1)} collective-permute-done((bf16[2,256,512]{2,1,0:T(8,128)(2,1)}, bf16[2,256,512]{2,1,0:T(8,128)(2,1)S(1)}, u32[]{:S(2)}, u32[]{:S(2)}) %collective-permute-start) | collective-permute-done | bytes 524320 | tf_op jit(solution)/shard_map/ppermute | solution.py:202
  55.6 0.0 copy-start
  55.6 0.8 %copy-done = bf16[2,256,512]{2,1,0:T(8,128)(2,1)} copy-done((bf16[2,256,512]{2,1,0:T(8,128)(2,1)}, bf16[2,256,512]{2,1,0:T(8,128)(2,1)S(1)}, u32[]{:S(2)}) %copy-start) | copy-done | bytes 524312
  56.4 12.8 %coupling.1 = bf16[2,2,8,256,2,256]{5,4,3,2,1,0:T(2,128)(2,1)} custom-call(bf16[2,256,512]{2,1,0:T(8,128)(2,1)} %transform.1.own_ref, bf16[2,256,512]{2,1,0:T(8,128)(2,1)} %copy-done, f32[8,8,256]{2,1,0:T(8,128)} %get-tuple-element.6.cos_ref, f32[8,8,256]{2,1,0:T(8,128)} %get-tuple-element.5.sin_ref), custom_call_target="tpu_custom_call" | custom-call | flops 4294967296 | bytes 10485760 | tf_op jit(solution)/shard_map/coupling/pallas_call | solution.py:206
  (1 shorter events, 0.0 us)
Async XLA Ops:
  37.8 17.8 %collective-permute-start = (bf16[2,256,512]{2,1,0:T(8,128)(2,1)}, bf16[2,256,512]{2,1,0:T(8,128)(2,1)S(1)}, u32[]{:S(2)}, u32[]{:S(2)}) collective-permute-start(bf16[2,256,512]{2,1,0:T(8,128)(2,1)} %transform.1.own_ref), channel_id=1, source_target_pairs={{1,0},{2,1},{3,2},{4,3},{5,4},{6,5},{7,6},{8,7},{9,8},{10,9},{11,1... | collective-permute-start | bytes 1572872 | tf_op jit(solution)/shard_map/ppermute | solution.py:202
  55.6 0.8 %copy-start = (bf16[2,256,512]{2,1,0:T(8,128)(2,1)}, bf16[2,256,512]{2,1,0:T(8,128)(2,1)S(1)}, u32[]{:S(2)}) copy-start(bf16[2,256,512]{2,1,0:T(8,128)(2,1)S(1)} %collective-permute-done.next_ref) | copy-start | bytes 1572868

commit v3 on v2

v3 whole, which is shorter than its diff:
```python
import math

import jax
import jax.numpy as jnp
import numpy as np
from jax import lax
from jax.experimental import pallas as pl
from jax.experimental.pallas import tpu as pltpu
from jax.sharding import PartitionSpec as P

BF = jnp.bfloat16
F32 = jnp.float32


def destination(chunk, slot):
    lat, core = slot >> 1, slot & 1
    return 2 * (chunk ^ (lat >> 2) ^ (lat & 3)) + core, lat


def longitude_table():
    chunk, op, slot = np.meshgrid(
        np.arange(4), np.arange(4), np.arange(32), indexing="ij"
    )
    tm, lat = destination(chunk, slot)
    order = (2 * (16 * tm + lat) + op // 2).reshape(-1)
    part = (op % 2).reshape(-1)
    phase = np.arange(1024)[:, None] * order[None, :] % 1024
    angle = phase * (2.0 * math.pi / 1024)
    table = np.where(part[None, :] == 0, np.cos(angle), -np.sin(angle))
    return jnp.asarray((table / 32.0).astype(np.float32)).astype(BF)


def swap_index_and_lanes(values, unit):
    values = list(values)
    lane = lax.broadcasted_iota(jnp.int32, values[0].shape, 1)
    step = len(values) // 2
    while step:
        low = (lane & (step * unit)) == 0
        for i in range(len(values)):
            if i & step == 0:
                a, b = values[i], values[i + step]
                values[i] = jnp.where(low, a, pltpu.roll(b, step * unit, 1))
                values[i + step] = jnp.where(
                    low, pltpu.roll(a, 128 - step * unit, 1), b
                )
        step //= 2
    return values


def transform_kernel(
    range_ref,
    x_hbm,
    table_hbm,
    proj_hbm,
    h_ref,
    x_ref,
    table_ref,
    proj_ref,
    flip_ref,
    s_ref,
    r_ref,
    a_ref,
    x_sem,
    table_sem,
    proj_sem,
    send_sem,
    recv_sem,
    pass_send_sem,
    pass_recv_sem,
):
    tm, lat = lax.axis_index("tm"), lax.axis_index("lat")
    me = 16 * tm + lat

    x_copies, table_copies = [], []
    for j in range(8):
        lanes = pl.ds(128 * j, 128)
        x_copies.append(
            pltpu.make_async_copy(x_hbm.at[:, :, lanes], x_ref.at[j], x_sem.at[j])
        )
    for j in range(2):
        lanes = pl.ds(256 * j, 256)
        table_copies.append(
            pltpu.make_async_copy(
                table_hbm.at[:, lanes], table_ref.at[j], table_sem.at[j]
            )
        )
    proj_copy = pltpu.make_async_copy(proj_hbm, proj_ref, proj_sem)
    table_copies[0].start()
    for copy in x_copies:
        copy.start()
    table_copies[1].start()
    proj_copy.start()

    barrier = pltpu.get_barrier_semaphore()

    @pl.loop(1, 128, unroll=4)
    def _(i):
        pl.semaphore_signal(barrier, inc=1, device_id=(tm ^ (i >> 4), lat ^ (i & 15)))

    table_copies[0].wait()
    for copy in x_copies:
        copy.wait()
    for gp in range(2):
        if gp == 1:
            table_copies[1].wait()
        for bh in range(2):
            rows = slice(16 * bh, 16 * bh + 16)
            x = jnp.concatenate(
                [x_ref[j, :, rows, :].reshape(512, 128) for j in range(8)], axis=1
            )
            z = jnp.dot(x, table_ref[gp], preferred_element_type=F32)
            z = z.astype(BF).reshape(32, 16, 256)
            for c in range(2):
                v = [z[t, :, 128 * c : 128 * c + 128] for t in range(32)]
                v = swap_index_and_lanes(v, 1)
                for slot in range(32):
                    s_ref[32 * (2 * gp + c) + slot, rows, :] = v[slot]
        if gp == 0:
            pl.semaphore_wait(barrier, 127)

        @pl.loop(0, 64, unroll=4)
        def _(i):
            chunk, slot = 2 * gp + (i & 1), (i >> 1) ^ (2 * lat + (tm & 1))
            to_tm, to_lat = destination(chunk, slot)

            @pl.when((to_tm != tm) | (to_lat != lat))
            def _():
                pltpu.make_async_remote_copy(
                    src_ref=s_ref.at[32 * chunk + slot],
                    dst_ref=r_ref.at[me],
                    send_sem=send_sem,
                    recv_sem=recv_sem,
                    device_id=(to_tm, to_lat),
                ).start()

    mine = 32 * ((tm >> 1) ^ (lat >> 2) ^ (lat & 3)) + 2 * lat + (tm & 1)
    r_ref[me] = s_ref[mine]
    proj_copy.wait()
    for o in range(2):
        flip_ref[o] = proj_ref[o].T
    rest = pltpu.make_async_remote_copy(
        src_ref=s_ref.at[pl.ds(0, 127)],
        dst_ref=r_ref.at[pl.ds(0, 127)],
        send_sem=send_sem,
        recv_sem=recv_sem,
        device_id=(tm, lat),
    )
    rest.wait_recv()

    for i in range(32):
        rows = slice(16 * i, 16 * i + 16)
        for q in range(2):
            v = [
                r_ref[16 * (4 * q + j) + i // 2, 16 * (i % 2) : 16 * (i % 2) + 16, :]
                for j in range(4)
            ]
            v = swap_index_and_lanes(v, 32)
            for op in range(4):
                a_ref[op // 2, 2 * (op % 2) + q, rows, :] = v[op]
    degree = lax.broadcasted_iota(jnp.int32, (256, 512), 0)
    before = jnp.maximum(me - 1, 0)
    passes = []
    for o in range(2):
        columns = jnp.concatenate([a_ref[o, j] for j in range(4)], axis=1)
        h = jnp.dot(flip_ref[o], columns, preferred_element_type=F32)
        low, high = range_ref[0, 2 * me + o], range_ref[1, 2 * me + o]
        keep = (degree >= low) & (degree < high)
        h_ref[o] = jnp.where(keep, h, 0.0).astype(BF)
        copy = pltpu.make_async_remote_copy(
            src_ref=h_ref.at[o],
            dst_ref=h_ref.at[2 + o],
            send_sem=pass_send_sem.at[o],
            recv_sem=pass_recv_sem.at[o],
            device_id=(before >> 4, before & 15),
        )
        passes.append(copy)

        @pl.when(me > 0)
        def _():
            copy.start()

    rest.wait_send()

    @pl.when(me == 127)
    def _():
        h_ref[2] = jnp.zeros((256, 512), BF)
        h_ref[3] = jnp.zeros((256, 512), BF)

    @pl.when(me < 127)
    def _():
        for copy in passes:
            copy.wait_recv()

    @pl.when(me > 0)
    def _():
        for copy in passes:
            copy.wait_send()


def phases(offset):
    row = lax.broadcasted_iota(jnp.int32, (8, 256), 0)
    t = lax.broadcasted_iota(jnp.int32, (8, 256), 1)
    turn = (offset * t + 64 * (row & 1)) & 255
    angle = turn.astype(F32) * (2.0 * math.pi / 256)
    return jnp.cos(angle) * (1.0 / 16), jnp.sin(angle) * (1.0 / 16)


def coupling_kernel(
    offsets_ref, h_ref, out_ref, twice_ref, cos_ref, sin_ref, left_ref
):
    o, pair = pl.program_id(0), pl.program_id(1)

    def build(slot, k):
        cos = jnp.broadcast_to(cos_ref[k][None], (64, 8, 256)).reshape(512, 256)
        sin = jnp.broadcast_to(sin_ref[k][None], (64, 8, 256)).reshape(512, 256)
        real, imag = twice_ref[:, :256], twice_ref[:, 256:]
        left_ref[slot, :, :256] = (real * cos - imag * sin).astype(BF)
        left_ref[slot, :, 256:] = (real * sin + imag * cos).astype(BF)

    def multiply(slot):
        for s in range(2):
            product = lax.dot_general(
                left_ref[slot],
                h_ref[o + 1 + s],
                (((1,), (1,)), ((), ())),
                preferred_element_type=F32,
            )
            out_ref[0, s, slot] = product.astype(BF).reshape(256, 2, 256)

    @pl.when((o == 0) & (pair == 0))
    def _():
        for k in range(8):
            cos, sin = phases(offsets_ref[k])
            cos_ref[k] = cos
            sin_ref[k] = sin

    @pl.when(pair == 0)
    def _():
        row = lax.broadcasted_iota(jnp.int32, (512, 256), 0)
        column = lax.broadcasted_iota(jnp.int32, (512, 256), 1)
        double = ((row >> 1) == column).astype(F32).astype(BF)
        twice_ref[...] = jnp.dot(double, h_ref[o], preferred_element_type=F32)
        build(0, 0)

    build(1, 2 * pair + 1)
    multiply(0)
    build(0, jnp.minimum(2 * pair + 2, 7))
    multiply(1)


def shards(frames, projection, degree_range, offsets):
    anywhere = pl.BlockSpec(memory_space=pl.ANY)
    spectra = pl.pallas_call(
        transform_kernel,
        in_specs=[pl.BlockSpec(memory_space=pltpu.SMEM)] + [anywhere] * 3,
        out_specs=pl.BlockSpec(memory_space=pltpu.VMEM),
        out_shape=jax.ShapeDtypeStruct((4, 256, 512), BF),
        scratch_shapes=[
            pltpu.VMEM((8, 32, 32, 128), BF),
            pltpu.VMEM((2, 1024, 256), BF),
            pltpu.VMEM((2, 512, 256), BF),
            pltpu.VMEM((2, 256, 512), BF),
            pltpu.VMEM((128, 32, 128), BF),
            pltpu.VMEM((128, 32, 128), BF),
            pltpu.VMEM((2, 4, 512, 128), BF),
            pltpu.SemaphoreType.DMA((8,)),
            pltpu.SemaphoreType.DMA((2,)),
            pltpu.SemaphoreType.DMA,
            pltpu.SemaphoreType.DMA,
            pltpu.SemaphoreType.DMA,
            pltpu.SemaphoreType.DMA((2,)),
            pltpu.SemaphoreType.DMA((2,)),
        ],
        compiler_params=pltpu.CompilerParams(collective_id=0, has_side_effects=True),
        cost_estimate=pl.CostEstimate(
            flops=2**30, bytes_accessed=4 << 20, transcendentals=0
        ),
        name="transform",
    )(degree_range.T, frames, longitude_table(), projection)
    return pl.pallas_call(
        coupling_kernel,
        grid=(2, 4),
        in_specs=[
            pl.BlockSpec(memory_space=pltpu.SMEM),
            pl.BlockSpec((4, 256, 512), lambda o, pair: (0, 0, 0)),
        ],
        out_specs=pl.BlockSpec(
            (1, 2, 2, 256, 2, 256), lambda o, pair: (o, 0, pair, 0, 0, 0)
        ),
        out_shape=jax.ShapeDtypeStruct((2, 2, 8, 256, 2, 256), BF),
        scratch_shapes=[
            pltpu.VMEM((512, 512), F32),
            pltpu.VMEM((8, 8, 256), F32),
            pltpu.VMEM((8, 8, 256), F32),
            pltpu.VMEM((2, 512, 512), BF),
        ],
        cost_estimate=pl.CostEstimate(
            flops=2**32, bytes_accessed=10 << 20, transcendentals=0
        ),
        name="coupling",
    )(offsets, spectra)


def solution(mesh):
    return jax.shard_map(
        shards,
        mesh=mesh,
        in_specs=(P("tm", "lat", None), P(("tm", "lat"), None, None), P(), P()),
        out_specs=P(("tm", "lat"), None, None, None, None, None),
        check_vma=False,
    )
```

time: 69.4 us -> 52.2 us (0.75)
  the two profiles are of different devices: /device:TPU:24 before, /device:TPU:95 now
where the time goes in v3:
time: 52.2 us; the launch traced here: 52.1 us
  Pallas kernels  52.1 us (100%)
    pallas_call x1, Pallas kernels, shards(): pl.pallas_call(transform_kernel, in_specs=[pl.BlockSpec(memory_space=pltp...  41.7 us
    pallas_call x1, Pallas kernels, shards(): pl.pallas_call(coupling_kernel, grid=(2, 4), in_specs=[pl.BlockSpec(memor...  10.4 us

profile of v3, /device:TPU:95, one launch (start us, length us, event | category | flops | bytes accessed | tf_op | source)
XLA Modules:
  0.0 52.1 jit_solution(7169331159051093247)
XLA Ops:
  0.0 41.7 %transform.1.h_ref = bf16[4,256,512]{2,1,0:T(8,128)(2,1)} custom-call(s32[2,256]{1,0:T(2,128)} %bitcast.1, bf16[32,32,1024]{2,1,0:T(8,128)(2,1)} %x_hbm.1, bf16[1024,512]{1,0:T(8,128)(2,1)} %constant.4.table_hbm, bf16[2,512,256]{2,1,0:T(8,128)(2,1)} %proj_hbm.1), custom_call_target="tpu_custom_call" | custom-call | flops 1073741824 | bytes 4194304 | tf_op jit(solution)/shard_map/transform/pallas_call | solution.py:253
  41.7 10.4 %coupling.1 = bf16[2,2,8,256,2,256]{5,4,3,2,1,0:T(2,128)(2,1)} custom-call(s32[8]{0:T(128)} %offsets_ref.1, bf16[4,256,512]{2,1,0:T(8,128)(2,1)} %transform.1.h_ref), custom_call_target="tpu_custom_call" | custom-call | flops 4294967296 | bytes 10485760 | tf_op jit(solution)/shard_map/coupling/pallas_call | solution.py:280

commit v4 on v3

--- a/solution.py
+++ b/solution.py
@@ -12,17 +12,11 @@
 F32 = jnp.float32
 
 
-def destination(chunk, slot):
-    lat, core = slot >> 1, slot & 1
-    return 2 * (chunk ^ (lat >> 2) ^ (lat & 3)) + core, lat
-
-
 def longitude_table():
-    chunk, op, slot = np.meshgrid(
+    group, op, slot = np.meshgrid(
         np.arange(4), np.arange(4), np.arange(32), indexing="ij"
     )
-    tm, lat = destination(chunk, slot)
-    order = (2 * (16 * tm + lat) + op // 2).reshape(-1)
+    order = (2 * (32 * group + slot) + op // 2).reshape(-1)
     part = (op % 2).reshape(-1)
     phase = np.arange(1024)[:, None] * order[None, :] % 1024
     angle = phase * (2.0 * math.pi / 1024)
@@ -57,7 +51,10 @@
     table_ref,
     proj_ref,
     flip_ref,
-    s_ref,
+    up_ref,
+    across_ref,
+    via_up_ref,
+    via_across_ref,
     r_ref,
     a_ref,
     x_sem,
@@ -72,41 +69,72 @@
     me = 16 * tm + lat
 
     x_copies, table_copies = [], []
-    for j in range(8):
-        lanes = pl.ds(128 * j, 128)
-        x_copies.append(
-            pltpu.make_async_copy(x_hbm.at[:, :, lanes], x_ref.at[j], x_sem.at[j])
-        )
+    for bh in range(2):
+        for j in range(8):
+            x_copies.append(
+                pltpu.make_async_copy(
+                    x_hbm.at[:, pl.ds(16 * bh, 16), pl.ds(128 * j, 128)],
+                    x_ref.at[bh, j],
+                    x_sem.at[bh, j],
+                )
+            )
     for j in range(2):
-        lanes = pl.ds(256 * j, 256)
         table_copies.append(
             pltpu.make_async_copy(
-                table_hbm.at[:, lanes], table_ref.at[j], table_sem.at[j]
+                table_hbm.at[:, pl.ds(256 * j, 256)], table_ref.at[j], table_sem.at[j]
             )
         )
     proj_copy = pltpu.make_async_copy(proj_hbm, proj_ref, proj_sem)
     table_copies[0].start()
-    for copy in x_copies:
+    for copy in x_copies[:8]:
         copy.start()
     table_copies[1].start()
+    for copy in x_copies[8:]:
+        copy.start()
     proj_copy.start()
 
     barrier = pltpu.get_barrier_semaphore()
-
-    @pl.loop(1, 128, unroll=4)
-    def _(i):
-        pl.semaphore_signal(barrier, inc=1, device_id=(tm ^ (i >> 4), lat ^ (i & 15)))
-
-    table_copies[0].wait()
-    for copy in x_copies:
-        copy.wait()
-    for gp in range(2):
-        if gp == 1:
-            table_copies[1].wait()
-        for bh in range(2):
-            rows = slice(16 * bh, 16 * bh + 16)
+    for i in range(1, 8):
+        pl.semaphore_signal(barrier, inc=1, device_id=(tm ^ i, lat))
+    for i in range(1, 16):
+        pl.semaphore_signal(barrier, inc=1, device_id=(tm, lat ^ i))
+
+    @pl.when((lat == 0) & (tm > 0))
+    def _():
+        pl.semaphore_signal(barrier, inc=1, device_id=(tm - 1, 15))
+
+    @pl.when((lat == 15) & (tm < 7))
+    def _():
+        pl.semaphore_signal(barrier, inc=1, device_id=(tm + 1, 0))
+
+    outside = ((lat == 0) & (tm > 0)) | ((lat == 15) & (tm < 7))
+
+    def up(i, source, target, stage):
+        return pltpu.make_async_remote_copy(
+            src_ref=source,
+            dst_ref=target,
+            send_sem=send_sem.at[stage],
+            recv_sem=recv_sem.at[stage],
+            device_id=(tm ^ i, lat),
+        )
+
+    def across(i, source, target, stage):
+        return pltpu.make_async_remote_copy(
+            src_ref=source,
+            dst_ref=target,
+            send_sem=send_sem.at[stage],
+            recv_sem=recv_sem.at[stage],
+            device_id=(tm, lat ^ i),
+        )
+
+    for bh in range(2):
+        for copy in x_copies[8 * bh : 8 * bh + 8]:
+            copy.wait()
+        for gp in range(2):
+            if bh == 0:
+                table_copies[gp].wait()
             x = jnp.concatenate(
-                [x_ref[j, :, rows, :].reshape(512, 128) for j in range(8)], axis=1
+                [x_ref[bh, j].reshape(512, 128) for j in range(8)], axis=1
             )
             z = jnp.dot(x, table_ref[gp], preferred_element_type=F32)
             z = z.astype(BF).reshape(32, 16, 256)
@@ -114,49 +142,54 @@
                 v = [z[t, :, 128 * c : 128 * c + 128] for t in range(32)]
                 v = swap_index_and_lanes(v, 1)
                 for slot in range(32):
-                    s_ref[32 * (2 * gp + c) + slot, rows, :] = v[slot]
-        if gp == 0:
-            pl.semaphore_wait(barrier, 127)
-
-        @pl.loop(0, 64, unroll=4)
-        def _(i):
-            chunk, slot = 2 * gp + (i & 1), (i >> 1) ^ (2 * lat + (tm & 1))
-            to_tm, to_lat = destination(chunk, slot)
-
-            @pl.when((to_tm != tm) | (to_lat != lat))
-            def _():
-                pltpu.make_async_remote_copy(
-                    src_ref=s_ref.at[32 * chunk + slot],
-                    dst_ref=r_ref.at[me],
-                    send_sem=send_sem,
-                    recv_sem=recv_sem,
-                    device_id=(to_tm, to_lat),
-                ).start()
-
-    mine = 32 * ((tm >> 1) ^ (lat >> 2) ^ (lat & 3)) + 2 * lat + (tm & 1)
-    r_ref[me] = s_ref[mine]
+                    to_tm, to_lat = 2 * (2 * gp + c) + slot // 16, slot % 16
+                    if bh == 0:
+                        up_ref[to_tm, to_lat] = v[slot]
+                    else:
+                        across_ref[to_lat, to_tm] = v[slot]
+        if bh == 0:
+            pl.semaphore_wait(barrier, 22 + outside.astype(jnp.int32))
+            for i in range(1, 8):
+                up(i, up_ref.at[tm ^ i], via_up_ref.at[tm], 0).start()
+            via_up_ref[tm] = up_ref[tm]
+        else:
+            for i in range(1, 16):
+                across(i, across_ref.at[lat ^ i], via_across_ref.at[lat], 1).start()
+            via_across_ref[lat] = across_ref[lat]
+
     proj_copy.wait()
     for o in range(2):
         flip_ref[o] = proj_ref[o].T
-    rest = pltpu.make_async_remote_copy(
-        src_ref=s_ref.at[pl.ds(0, 127)],
-        dst_ref=r_ref.at[pl.ds(0, 127)],
-        send_sem=send_sem,
-        recv_sem=recv_sem,
-        device_id=(tm, lat),
+
+    first = pl.ds(0, 7)
+    up_all = up(0, up_ref.at[first], via_up_ref.at[first], 0)
+    up_all.wait_recv()
+    for i in range(1, 16):
+        across(i, via_up_ref.at[:, lat ^ i], r_ref.at[:, lat, 0], 2).start()
+    r_ref[:, lat, 0] = via_up_ref[:, lat]
+    first = pl.ds(0, 15)
+    across_all = across(0, across_ref.at[first], via_across_ref.at[first], 1)
+    across_all.wait_recv()
+    for i in range(1, 8):
+        up(i, via_across_ref.at[:, tm ^ i], r_ref.at[tm, :, 1], 3).start()
+    r_ref[tm, :, 1] = via_across_ref[:, tm]
+
+    across_last = across(
+        0, via_across_ref.at[pl.ds(0, 15)], r_ref.at[:, pl.ds(0, 15), 0], 2
     )
-    rest.wait_recv()
-
-    for i in range(32):
-        rows = slice(16 * i, 16 * i + 16)
-        for q in range(2):
-            v = [
-                r_ref[16 * (4 * q + j) + i // 2, 16 * (i % 2) : 16 * (i % 2) + 16, :]
-                for j in range(4)
-            ]
-            v = swap_index_and_lanes(v, 32)
-            for op in range(4):
-                a_ref[op // 2, 2 * (op % 2) + q, rows, :] = v[op]
+    up_last = up(0, via_up_ref.at[pl.ds(0, 7)], r_ref.at[pl.ds(0, 7), :, 1], 3)
+    for half in range(2):
+        if half == 0:
+            across_last.wait_recv()
+        else:
+            up_last.wait_recv()
+        for i in range(16):
+            rows = slice(32 * i + 16 * half, 32 * i + 16 * half + 16)
+            for q in range(2):
+                v = [r_ref[4 * q + j, i, half] for j in range(4)]
+                v = swap_index_and_lanes(v, 32)
+                for op in range(4):
+                    a_ref[op // 2, 2 * (op % 2) + q, rows, :] = v[op]
     degree = lax.broadcasted_iota(jnp.int32, (256, 512), 0)
     before = jnp.maximum(me - 1, 0)
     passes = []
@@ -179,7 +212,10 @@
         def _():
             copy.start()
 
-    rest.wait_send()
+    up_all.wait_send()
+    across_all.wait_send()
+    across_last.wait_send()
+    up_last.wait_send()
 
     @pl.when(me == 127)
     def _():
@@ -256,18 +292,21 @@
         out_specs=pl.BlockSpec(memory_space=pltpu.VMEM),
         out_shape=jax.ShapeDtypeStruct((4, 256, 512), BF),
         scratch_shapes=[
-            pltpu.VMEM((8, 32, 32, 128), BF),
+            pltpu.VMEM((2, 8, 32, 16, 128), BF),
             pltpu.VMEM((2, 1024, 256), BF),
             pltpu.VMEM((2, 512, 256), BF),
             pltpu.VMEM((2, 256, 512), BF),
-            pltpu.VMEM((128, 32, 128), BF),
-            pltpu.VMEM((128, 32, 128), BF),
+            pltpu.VMEM((8, 16, 16, 128), BF),
+            pltpu.VMEM((16, 8, 16, 128), BF),
+            pltpu.VMEM((8, 16, 16, 128), BF),
+            pltpu.VMEM((16, 8, 16, 128), BF),
+            pltpu.VMEM((8, 16, 2, 16, 128), BF),
             pltpu.VMEM((2, 4, 512, 128), BF),
-            pltpu.SemaphoreType.DMA((8,)),
+            pltpu.SemaphoreType.DMA((2, 8)),
             pltpu.SemaphoreType.DMA((2,)),
             pltpu.SemaphoreType.DMA,
-            pltpu.SemaphoreType.DMA,
-            pltpu.SemaphoreType.DMA,
+            pltpu.SemaphoreType.DMA((4,)),
+            pltpu.SemaphoreType.DMA((4,)),
             pltpu.SemaphoreType.DMA((2,)),
             pltpu.SemaphoreType.DMA((2,)),
         ],

time: 52.2 us -> 53.2 us (1.019)
  the two profiles are of different devices: /device:TPU:95 before, /device:TPU:0 now
where the time goes in v4:
time: 53.2 us; the launch traced here: 53 us
  Pallas kernels  53 us (100%)
    pallas_call x1, Pallas kernels, shards(): pl.pallas_call(transform_kernel, in_specs=[pl.BlockSpec(memory_space=pltp...  42.6 us
    pallas_call x1, Pallas kernels, shards(): pl.pallas_call(coupling_kernel, grid=(2, 4), in_specs=[pl.BlockSpec(memor...  10.4 us

profile of v4, /device:TPU:0, one launch (start us, length us, event | category | flops | bytes accessed | tf_op | source)
XLA Modules:
  0.0 53.0 jit_solution(13145373523746325432)
XLA Ops:
  0.0 42.6 %transform.1.h_ref = bf16[4,256,512]{2,1,0:T(8,128)(2,1)} custom-call(s32[2,256]{1,0:T(2,128)} %bitcast.1, bf16[32,32,1024]{2,1,0:T(8,128)(2,1)} %x_hbm.1, bf16[1024,512]{1,0:T(8,128)(2,1)} %constant.4.table_hbm, bf16[2,512,256]{2,1,0:T(8,128)(2,1)} %proj_hbm.1), custom_call_target="tpu_custom_call" | custom-call | flops 1073741824 | bytes 4194304 | tf_op jit(solution)/shard_map/transform/pallas_call | solution.py:289
  42.6 10.4 %coupling.1 = bf16[2,2,8,256,2,256]{5,4,3,2,1,0:T(2,128)(2,1)} custom-call(s32[8]{0:T(128)} %offsets_ref.1, bf16[4,256,512]{2,1,0:T(8,128)(2,1)} %transform.1.h_ref), custom_call_target="tpu_custom_call" | custom-call | flops 4294967296 | bytes 10485760 | tf_op jit(solution)/shard_map/coupling/pallas_call | solution.py:319

commit v5 on v4

--- a/solution.py
+++ b/solution.py
@@ -22,6 +22,17 @@
     angle = phase * (2.0 * math.pi / 1024)
     table = np.where(part[None, :] == 0, np.cos(angle), -np.sin(angle))
     return jnp.asarray((table / 32.0).astype(np.float32)).astype(BF)
+
+
+def farthest_first(count, fields):
+    def hops(i):
+        return sum((0, 1, 2, 1)[i >> shift & 3] for shift in fields)
+
+    return sorted(range(1, count), key=lambda i: (-hops(i), i))
+
+
+UP = farthest_first(8, (1,))
+ACROSS = farthest_first(16, (0, 2))
 
 
 def swap_index_and_lanes(values, unit):
@@ -43,10 +54,12 @@
 
 def transform_kernel(
     range_ref,
+    offsets_ref,
     x_hbm,
     table_hbm,
     proj_hbm,
     h_ref,
+    left_ref,
     x_ref,
     table_ref,
     proj_ref,
@@ -57,6 +70,7 @@
     via_across_ref,
     r_ref,
     a_ref,
+    twice_ref,
     x_sem,
     table_sem,
     proj_sem,
@@ -147,31 +161,31 @@
                         up_ref[to_tm, to_lat] = v[slot]
                     else:
                         across_ref[to_lat, to_tm] = v[slot]
-        if bh == 0:
-            pl.semaphore_wait(barrier, 22 + outside.astype(jnp.int32))
-            for i in range(1, 8):
-                up(i, up_ref.at[tm ^ i], via_up_ref.at[tm], 0).start()
-            via_up_ref[tm] = up_ref[tm]
-        else:
-            for i in range(1, 16):
-                across(i, across_ref.at[lat ^ i], via_across_ref.at[lat], 1).start()
-            via_across_ref[lat] = across_ref[lat]
+    pl.semaphore_wait(barrier, 22 + outside.astype(jnp.int32))
+    for i in ACROSS[:8]:
+        across(i, across_ref.at[lat ^ i], via_across_ref.at[lat], 1).start()
+    for i in UP:
+        up(i, up_ref.at[tm ^ i], via_up_ref.at[tm], 0).start()
+    for i in ACROSS[8:]:
+        across(i, across_ref.at[lat ^ i], via_across_ref.at[lat], 1).start()
+    via_up_ref[tm] = up_ref[tm]
+    via_across_ref[lat] = across_ref[lat]
 
     proj_copy.wait()
     for o in range(2):
         flip_ref[o] = proj_ref[o].T
 
-    first = pl.ds(0, 7)
-    up_all = up(0, up_ref.at[first], via_up_ref.at[first], 0)
+    some = pl.ds(0, 7)
+    up_all = up(0, up_ref.at[some], via_up_ref.at[some], 0)
     up_all.wait_recv()
-    for i in range(1, 16):
+    for i in ACROSS:
         across(i, via_up_ref.at[:, lat ^ i], r_ref.at[:, lat, 0], 2).start()
+    some = pl.ds(0, 15)
+    across_all = across(0, across_ref.at[some], via_across_ref.at[some], 1)
+    across_all.wait_recv()
+    for i in UP:
+        up(i, via_across_ref.at[:, tm ^ i], r_ref.at[tm, :, 1], 3).start()
     r_ref[:, lat, 0] = via_up_ref[:, lat]
-    first = pl.ds(0, 15)
-    across_all = across(0, across_ref.at[first], via_across_ref.at[first], 1)
-    across_all.wait_recv()
-    for i in range(1, 8):
-        up(i, via_across_ref.at[:, tm ^ i], r_ref.at[tm, :, 1], 3).start()
     r_ref[tm, :, 1] = via_across_ref[:, tm]
 
     across_last = across(
@@ -192,45 +206,65 @@
                     a_ref[op // 2, 2 * (op % 2) + q, rows, :] = v[op]
     degree = lax.broadcasted_iota(jnp.int32, (256, 512), 0)
     before = jnp.maximum(me - 1, 0)
-    passes = []
+
+    def passed(o, c):
+        rows = pl.ds(32 * c, 32)
+        return pltpu.make_async_remote_copy(
+            src_ref=h_ref.at[o, rows],
+            dst_ref=h_ref.at[2 + o, rows],
+            send_sem=pass_send_sem.at[o, c],
+            recv_sem=pass_recv_sem.at[o, c],
+            device_id=(before >> 4, before & 15),
+        )
+
     for o in range(2):
         columns = jnp.concatenate([a_ref[o, j] for j in range(4)], axis=1)
         h = jnp.dot(flip_ref[o], columns, preferred_element_type=F32)
         low, high = range_ref[0, 2 * me + o], range_ref[1, 2 * me + o]
         keep = (degree >= low) & (degree < high)
         h_ref[o] = jnp.where(keep, h, 0.0).astype(BF)
-        copy = pltpu.make_async_remote_copy(
-            src_ref=h_ref.at[o],
-            dst_ref=h_ref.at[2 + o],
-            send_sem=pass_send_sem.at[o],
-            recv_sem=pass_recv_sem.at[o],
-            device_id=(before >> 4, before & 15),
-        )
-        passes.append(copy)
-
-        @pl.when(me > 0)
-        def _():
-            copy.start()
+        for c in range(8):
+
+            @pl.when((me > 0) & (32 * (c + 1) > 2 * me + o))
+            def _():
+                passed(o, c).start()
 
     up_all.wait_send()
     across_all.wait_send()
     across_last.wait_send()
     up_last.wait_send()
 
-    @pl.when(me == 127)
-    def _():
-        h_ref[2] = jnp.zeros((256, 512), BF)
-        h_ref[3] = jnp.zeros((256, 512), BF)
-
-    @pl.when(me < 127)
-    def _():
-        for copy in passes:
-            copy.wait_recv()
-
-    @pl.when(me > 0)
-    def _():
-        for copy in passes:
-            copy.wait_send()
+    row = lax.broadcasted_iota(jnp.int32, (512, 256), 0)
+    column = lax.broadcasted_iota(jnp.int32, (512, 256), 1)
+    double = ((row >> 1) == column).astype(F32).astype(BF)
+    for o in range(2):
+        twice_ref[o] = jnp.dot(double, h_ref[o], preferred_element_type=F32)
+
+    @pl.loop(0, 8)
+    def _(k):
+        cos, sin = phases(offsets_ref[k])
+        cos = jnp.broadcast_to(cos[None], (64, 8, 256)).reshape(512, 256)
+        sin = jnp.broadcast_to(sin[None], (64, 8, 256)).reshape(512, 256)
+        for o in range(2):
+            real, imag = twice_ref[o, :, :256], twice_ref[o, :, 256:]
+            left_ref[o, k, :, :256] = (real * cos - imag * sin).astype(BF)
+            left_ref[o, k, :, 256:] = (real * sin + imag * cos).astype(BF)
+
+    for o in range(2):
+        for c in range(8):
+            sent = (me < 127) & (32 * (c + 1) > 2 * (me + 1) + o)
+
+            @pl.when(sent)
+            def _():
+                passed(o, c).wait_recv()
+
+            @pl.when(jnp.logical_not(sent))
+            def _():
+                h_ref[2 + o, 32 * c : 32 * c + 32] = jnp.zeros((32, 512), BF)
+
+            @pl.when((me > 0) & (32 * (c + 1) > 2 * me + o))
+            def _():
+                passed(o, c).wait_send()
 
 
 def phases(offset):
@@ -241,56 +275,32 @@
     return jnp.cos(angle) * (1.0 / 16), jnp.sin(angle) * (1.0 / 16)
 
 
-def coupling_kernel(
-    offsets_ref, h_ref, out_ref, twice_ref, cos_ref, sin_ref, left_ref
-):
-    o, pair = pl.program_id(0), pl.program_id(1)
-
-    def build(slot, k):
-        cos = jnp.broadcast_to(cos_ref[k][None], (64, 8, 256)).reshape(512, 256)
-        sin = jnp.broadcast_to(sin_ref[k][None], (64, 8, 256)).reshape(512, 256)
-        real, imag = twice_ref[:, :256], twice_ref[:, 256:]
-        left_ref[slot, :, :256] = (real * cos - imag * sin).astype(BF)
-        left_ref[slot, :, 256:] = (real * sin + imag * cos).astype(BF)
-
-    def multiply(slot):
-        for s in range(2):
-            product = lax.dot_general(
-                left_ref[slot],
-                h_ref[o + 1 + s],
-                (((1,), (1,)), ((), ())),
-                preferred_element_type=F32,
-            )
-            out_ref[0, s, slot] = product.astype(BF).reshape(256, 2, 256)
-
-    @pl.when((o == 0) & (pair == 0))
-    def _():
-        for k in range(8):
-            cos, sin = phases(offsets_ref[k])
-            cos_ref[k] = cos
-            sin_ref[k] = sin
-
-    @pl.when(pair == 0)
-    def _():
-        row = lax.broadcasted_iota(jnp.int32, (512, 256), 0)
-        column = lax.broadcasted_iota(jnp.int32, (512, 256), 1)
-        double = ((row >> 1) == column).astype(F32).astype(BF)
-        twice_ref[...] = jnp.dot(double, h_ref[o], preferred_element_type=F32)
-        build(0, 0)
-
-    build(1, 2 * pair + 1)
-    multiply(0)
-    build(0, jnp.minimum(2 * pair + 2, 7))
-    multiply(1)
+def coupling_kernel(left_ref, h_ref, out_ref):
+    o = pl.program_id(0)
+    for s in range(2):
+        product = lax.dot_general(
+            left_ref[0].reshape(1024, 512),
+            h_ref[o + 1 + s],
+            (((1,), (1,)), ((), ())),
+            preferred_element_type=F32,
+        )
+        out_ref[0, s] = product.astype(BF).reshape(2, 256, 2, 256)
 
 
 def shards(frames, projection, degree_range, offsets):
-    anywhere = pl.BlockSpec(memory_space=pl.ANY)
-    spectra = pl.pallas_call(
+    anywhere = pl.BlockSpec(memory_space=pltpu.HBM)
+    far = [
+        pltpu.with_memory_space_constraint(a, pltpu.HBM)
+        for a in (degree_range.T, offsets, frames, longitude_table(), projection)
+    ]
+    spectra, left = pl.pallas_call(
         transform_kernel,
-        in_specs=[pl.BlockSpec(memory_space=pltpu.SMEM)] + [anywhere] * 3,
-        out_specs=pl.BlockSpec(memory_space=pltpu.VMEM),
-        out_shape=jax.ShapeDtypeStruct((4, 256, 512), BF),
+        in_specs=[pl.BlockSpec(memory_space=pltpu.SMEM)] * 2 + [anywhere] * 3,
+        out_specs=[pl.BlockSpec(memory_space=pltpu.VMEM)] * 2,
+        out_shape=[
+            jax.ShapeDtypeStruct((4, 256, 512), BF),
+            jax.ShapeDtypeStruct((2, 8, 512, 512), BF),
+        ],
         scratch_shapes=[
             pltpu.VMEM((2, 8, 32, 16, 128), BF),
             pltpu.VMEM((2, 1024, 256), BF),
@@ -302,42 +312,40 @@
             pltpu.VMEM((16, 8, 16, 128), BF),
             pltpu.VMEM((8, 16, 2, 16, 128), BF),
             pltpu.VMEM((2, 4, 512, 128), BF),
+            pltpu.VMEM((2, 512, 512), F32),
             pltpu.SemaphoreType.DMA((2, 8)),
             pltpu.SemaphoreType.DMA((2,)),
             pltpu.SemaphoreType.DMA,
             pltpu.SemaphoreType.DMA((4,)),
             pltpu.SemaphoreType.DMA((4,)),
-            pltpu.SemaphoreType.DMA((2,)),
-            pltpu.SemaphoreType.DMA((2,)),
+            pltpu.SemaphoreType.DMA((2, 8)),
+            pltpu.SemaphoreType.DMA((2, 8)),
         ],
-        compiler_params=pltpu.CompilerParams(collective_id=0, has_side_effects=True),
+        compiler_params=pltpu.CompilerParams(
+            collective_id=0, has_side_effects=True, vmem_limit_bytes=26 << 20
+        ),
         cost_estimate=pl.CostEstimate(
             flops=2**30, bytes_accessed=4 << 20, transcendentals=0
         ),
         name="transform",
-    )(degree_range.T, frames, longitude_table(), projection)
+    )(*far)
     return pl.pallas_call(
         coupling_kernel,
         grid=(2, 4),
         in_specs=[
-            pl.BlockSpec(memory_space=pltpu.SMEM),
+            pl.BlockSpec((1, 2, 512, 512), lambda o, pair: (o, pair, 0, 0)),
             pl.BlockSpec((4, 256, 512), lambda o, pair: (0, 0, 0)),
         ],
         out_specs=pl.BlockSpec(
             (1, 2, 2, 256, 2, 256), lambda o, pair: (o, 0, pair, 0, 0, 0)
         ),
         out_shape=jax.ShapeDtypeStruct((2, 2, 8, 256, 2, 256), BF),
-        scratch_shapes=[
-            pltpu.VMEM((512, 512), F32),
-            pltpu.VMEM((8, 8, 256), F32),
-            pltpu.VMEM((8, 8, 256), F32),
-            pltpu.VMEM((2, 512, 512), BF),
-        ],
         cost_estimate=pl.CostEstimate(
             flops=2**32, bytes_accessed=10 << 20, transcendentals=0
         ),
+        compiler_params=pltpu.CompilerParams(vmem_limit_bytes=26 << 20),
         name="coupling",
-    )(offsets, spectra)
+    )(left, spectra)
 
 
 def solution(mesh):

time: 53.2 us -> 48.1 us (0.904)
  Pallas kernels: 53 us -> 48 us
    pallas_call x1, Pallas kernels: 42.6 us -> 40.1 us  [shards(): pl.pallas_call(transform_kernel, in_specs=[pl.BlockSpec(memory_space=pltp...]
    pallas_call x1, Pallas kernels: 10.4 us -> 7.91 us  [shards(): pl.pallas_call(coupling_kernel, grid=(2, 4), in_specs=[pl.BlockSpec((1, 2...]
where the time goes in v5:
time: 48.1 us; the launch traced here: 48 us
  Pallas kernels  48 us (100%)
    pallas_call x1, Pallas kernels, shards(): pl.pallas_call(transform_kernel, in_specs=[pl.BlockSpec(memory_space=pltp...  40.1 us
    pallas_call x1, Pallas kernels, shards(): pl.pallas_call(coupling_kernel, grid=(2, 4), in_specs=[pl.BlockSpec((1, 2...  7.91 us

profile of v5, /device:TPU:0, one launch (start us, length us, event | category | flops | bytes accessed | tf_op | source)
XLA Modules:
  0.0 48.0 jit_solution(9031994685472717317)
XLA Ops:
  0.0 40.1 %transform.1 = (bf16[4,256,512]{2,1,0:T(8,128)(2,1)S(1)}, bf16[2,8,512,512]{3,2,1,0:T(8,128)(2,1)S(1)}) custom-call(s32[2,256]{1,0:T(2,128)} %bitcast.1, s32[8]{0:T(128)} %offsets_ref.1, bf16[32,32,1024]{2,1,0:T(8,128)(2,1)} %x_hbm.1, bf16[1024,512]{1,0:T(8,128)(2,1)} %constant.4.table_hbm, bf16[2,512,256]{2,1,0:T(8,128)(2,1)} %proj_hbm.1), custom_call_target="tpu_custom_call" | custom-call | flops 1073741824 | bytes 4194304 | tf_op jit(solution)/shard_map/transform/pallas_call | solution.py:296
  40.1 7.9 %coupling.1 = bf16[2,2,8,256,2,256]{5,4,3,2,1,0:T(2,128)(2,1)} custom-call(bf16[2,8,512,512]{3,2,1,0:T(8,128)(2,1)S(1)} %get-tuple-element.7.left_ref, bf16[4,256,512]{2,1,0:T(8,128)(2,1)S(1)} %get-tuple-element.8.h_ref), custom_call_target="tpu_custom_call" | custom-call | flops 4294967296 | bytes 10485760 | tf_op jit(solution)/shard_map/coupling/pallas_call | solution.py:332

commit v6 on v5

--- a/solution.py
+++ b/solution.py
@@ -58,6 +58,7 @@
     x_hbm,
     table_hbm,
     proj_hbm,
+    out_ref,
     h_ref,
     left_ref,
     x_ref,
@@ -250,7 +251,19 @@
             left_ref[o, k, :, :256] = (real * cos - imag * sin).astype(BF)
             left_ref[o, k, :, 256:] = (real * sin + imag * cos).astype(BF)
 
-    for o in range(2):
+    def couple(o, s):
+        @pl.loop(0, 2)
+        def _(half):
+            for i in range(4):
+                product = lax.dot_general(
+                    left_ref[o, 4 * half + i],
+                    h_ref[o + 1 + s],
+                    (((1,), (1,)), ((), ())),
+                    preferred_element_type=F32,
+                )
+                out_ref[o, s, 4 * half + i] = product.astype(BF).reshape(256, 2, 256)
+
+    def receive(o):
         for c in range(8):
             sent = (me < 127) & (32 * (c + 1) > 2 * (me + 1) + o)
 
@@ -261,6 +274,15 @@
             @pl.when(jnp.logical_not(sent))
             def _():
                 h_ref[2 + o, 32 * c : 32 * c + 32] = jnp.zeros((32, 512), BF)
+
+    couple(0, 0)
+    receive(0)
+    couple(0, 1)
+    couple(1, 0)
+    receive(1)
+    couple(1, 1)
+    for o in range(2):
+        for c in range(8):
 
             @pl.when((me > 0) & (32 * (c + 1) > 2 * me + o))
             def _():
@@ -275,33 +297,20 @@
     return jnp.cos(angle) * (1.0 / 16), jnp.sin(angle) * (1.0 / 16)
 
 
-def coupling_kernel(left_ref, h_ref, out_ref):
-    o = pl.program_id(0)
-    for s in range(2):
-        product = lax.dot_general(
-            left_ref[0].reshape(1024, 512),
-            h_ref[o + 1 + s],
-            (((1,), (1,)), ((), ())),
-            preferred_element_type=F32,
-        )
-        out_ref[0, s] = product.astype(BF).reshape(2, 256, 2, 256)
-
-
 def shards(frames, projection, degree_range, offsets):
     anywhere = pl.BlockSpec(memory_space=pltpu.HBM)
     far = [
         pltpu.with_memory_space_constraint(a, pltpu.HBM)
         for a in (degree_range.T, offsets, frames, longitude_table(), projection)
     ]
-    spectra, left = pl.pallas_call(
+    return pl.pallas_call(
         transform_kernel,
         in_specs=[pl.BlockSpec(memory_space=pltpu.SMEM)] * 2 + [anywhere] * 3,
-        out_specs=[pl.BlockSpec(memory_space=pltpu.VMEM)] * 2,
-        out_shape=[
-            jax.ShapeDtypeStruct((4, 256, 512), BF),
-            jax.ShapeDtypeStruct((2, 8, 512, 512), BF),
-        ],
+        out_specs=pl.BlockSpec(memory_space=pltpu.VMEM),
+        out_shape=jax.ShapeDtypeStruct((2, 2, 8, 256, 2, 256), BF),
         scratch_shapes=[
+            pltpu.VMEM((4, 256, 512), BF),
+            pltpu.VMEM((2, 8, 512, 512), BF),
             pltpu.VMEM((2, 8, 32, 16, 128), BF),
             pltpu.VMEM((2, 1024, 256), BF),
             pltpu.VMEM((2, 512, 256), BF),
@@ -322,30 +331,13 @@
             pltpu.SemaphoreType.DMA((2, 8)),
         ],
         compiler_params=pltpu.CompilerParams(
-            collective_id=0, has_side_effects=True, vmem_limit_bytes=26 << 20
+            collective_id=0, has_side_effects=True, vmem_limit_bytes=36 << 20
         ),
         cost_estimate=pl.CostEstimate(
-            flops=2**30, bytes_accessed=4 << 20, transcendentals=0
+            flops=2**32, bytes_accessed=12 << 20, transcendentals=0
         ),
         name="transform",
     )(*far)
-    return pl.pallas_call(
-        coupling_kernel,
-        grid=(2, 4),
-        in_specs=[
-            pl.BlockSpec((1, 2, 512, 512), lambda o, pair: (o, pair, 0, 0)),
-            pl.BlockSpec((4, 256, 512), lambda o, pair: (0, 0, 0)),
-        ],
-        out_specs=pl.BlockSpec(
-            (1, 2, 2, 256, 2, 256), lambda o, pair: (o, 0, pair, 0, 0, 0)
-        ),
-        out_shape=jax.ShapeDtypeStruct((2, 2, 8, 256, 2, 256), BF),
-        cost_estimate=pl.CostEstimate(
-            flops=2**32, bytes_accessed=10 << 20, transcendentals=0
-        ),
-        compiler_params=pltpu.CompilerParams(vmem_limit_bytes=26 << 20),
-        name="coupling",
-    )(left, spectra)
 
 
 def solution(mesh):

time: 48.1 us -> 45.3 us (0.942)
  Pallas kernels: 48 us -> 41.7 us
  local copies, waits for them, and re-layouts: 0 us -> 3.4 us
    pallas_call x1 -> x0, Pallas kernels: 7.91 us -> none  [shards(): pl.pallas_call(coupling_kernel, grid=(2, 4), in_specs=[pl.BlockSpec((1, 2...]
    unnamed x0 -> x1, local copies, waits for them, and re-layouts: none -> 3.4 us
    pallas_call x1, Pallas kernels: 40.1 us -> 41.7 us  [shards(): pl.pallas_call(transform_kernel, in_specs=[pl.BlockSpec(memory_space=pltp...]
where the time goes in v6:
time: 45.3 us; the launch traced here: 45.1 us
  Pallas kernels  41.7 us (92%)
  local copies, waits for them, and re-layouts  3.4 us (8%)
    pallas_call x1, Pallas kernels, shards(): pl.pallas_call(transform_kernel, in_specs=[pl.BlockSpec(memory_space=pltp...  41.7 us
    unnamed x1, local copies, waits for them, and re-layouts  3.4 us

profile of v6, /device:TPU:0, one launch (start us, length us, event | category | flops | bytes accessed | tf_op | source)
XLA Modules:
  0.0 45.1 jit_solution(16493629970285548044)
XLA Ops:
  0.0 41.7 %transform.1 = bf16[2,2,8,256,2,256]{5,4,3,2,1,0:T(2,128)(2,1)S(1)} custom-call(s32[2,256]{1,0:T(2,128)} %bitcast.1, s32[8]{0:T(128)} %offsets_ref.1, bf16[32,32,1024]{2,1,0:T(8,128)(2,1)} %x_hbm.1, bf16[1024,512]{1,0:T(8,128)(2,1)} %constant.4.table_hbm, bf16[2,512,256]{2,1,0:T(8,128)(2,1)} %proj_hbm.1), custom_call_target="tpu_custom_call" | custom-call | flops 4294967296 | bytes 12582912 | tf_op jit(solution)/shard_map/transform/pallas_call | solution.py:306
  41.7 3.4 %copy.7 = bf16[2,2,8,256,2,256]{5,4,3,2,1,0:T(2,128)(2,1)} copy(bf16[2,2,8,256,2,256]{5,4,3,2,1,0:T(2,128)(2,1)S(1)} %transform.1) | data formatting | bytes 16777216

commit v7 on v6

--- a/solution.py
+++ b/solution.py
@@ -59,8 +59,10 @@
     table_hbm,
     proj_hbm,
     out_ref,
+    last_ref,
+    left_ref,
     h_ref,
-    left_ref,
+    left0_ref,
     x_ref,
     table_ref,
     proj_ref,
@@ -241,27 +243,31 @@
     for o in range(2):
         twice_ref[o] = jnp.dot(double, h_ref[o], preferred_element_type=F32)
 
-    @pl.loop(0, 8)
-    def _(k):
+    def build(o, k, target):
         cos, sin = phases(offsets_ref[k])
         cos = jnp.broadcast_to(cos[None], (64, 8, 256)).reshape(512, 256)
         sin = jnp.broadcast_to(sin[None], (64, 8, 256)).reshape(512, 256)
-        for o in range(2):
-            real, imag = twice_ref[o, :, :256], twice_ref[o, :, 256:]
-            left_ref[o, k, :, :256] = (real * cos - imag * sin).astype(BF)
-            left_ref[o, k, :, 256:] = (real * sin + imag * cos).astype(BF)
-
-    def couple(o, s):
+        real, imag = twice_ref[o, :, :256], twice_ref[o, :, 256:]
+        target[k, :, :256] = (real * cos - imag * sin).astype(BF)
+        target[k, :, 256:] = (real * sin + imag * cos).astype(BF)
+
+    @pl.loop(0, 8)
+    def _(k):
+        build(0, k, left0_ref)
+
+    def couple(place, left, partner, with_build=False):
         @pl.loop(0, 2)
         def _(half):
             for i in range(4):
+                if with_build:
+                    build(1, 4 * half + i, left_ref)
                 product = lax.dot_general(
-                    left_ref[o, 4 * half + i],
-                    h_ref[o + 1 + s],
+                    left[4 * half + i],
+                    h_ref[partner],
                     (((1,), (1,)), ((), ())),
                     preferred_element_type=F32,
                 )
-                out_ref[o, s, 4 * half + i] = product.astype(BF).reshape(256, 2, 256)
+                out_ref[place, 4 * half + i] = product.astype(BF).reshape(256, 2, 256)
 
     def receive(o):
         for c in range(8):
@@ -275,12 +281,12 @@
             def _():
                 h_ref[2 + o, 32 * c : 32 * c + 32] = jnp.zeros((32, 512), BF)
 
-    couple(0, 0)
+    couple(0, left0_ref, 1, with_build=True)
     receive(0)
-    couple(0, 1)
-    couple(1, 0)
+    couple(1, left0_ref, 2)
+    couple(2, left_ref, 2)
     receive(1)
-    couple(1, 1)
+    last_ref[...] = h_ref[3]
     for o in range(2):
         for c in range(8):
 
@@ -297,20 +303,56 @@
     return jnp.cos(angle) * (1.0 / 16), jnp.sin(angle) * (1.0 / 16)
 
 
+def finish_kernel(out_ref, last_ref, left_ref, out_hbm, block_ref, early_sem, late_sem):
+    early = [
+        pltpu.make_async_copy(out_ref.at[i], out_hbm.at[o, s], early_sem.at[i])
+        for i, (o, s) in enumerate(((0, 0), (0, 1), (1, 0)))
+    ]
+    for copy in early:
+        copy.start()
+
+    def late(half):
+        some = pl.ds(4 * half, 4)
+        return pltpu.make_async_copy(
+            block_ref.at[some], out_hbm.at[1, 1, some], late_sem.at[half]
+        )
+
+    @pl.loop(0, 2)
+    def _(half):
+        for i in range(4):
+            product = lax.dot_general(
+                left_ref[4 * half + i],
+                last_ref[...],
+                (((1,), (1,)), ((), ())),
+                preferred_element_type=F32,
+            )
+            block_ref[4 * half + i] = product.astype(BF).reshape(256, 2, 256)
+        late(half).start()
+
+    for copy in early:
+        copy.wait()
+    for half in range(2):
+        late(half).wait()
+
+
 def shards(frames, projection, degree_range, offsets):
     anywhere = pl.BlockSpec(memory_space=pltpu.HBM)
     far = [
         pltpu.with_memory_space_constraint(a, pltpu.HBM)
         for a in (degree_range.T, offsets, frames, longitude_table(), projection)
     ]
-    return pl.pallas_call(
+    ready, last, left = pl.pallas_call(
         transform_kernel,
         in_specs=[pl.BlockSpec(memory_space=pltpu.SMEM)] * 2 + [anywhere] * 3,
-        out_specs=pl.BlockSpec(memory_space=pltpu.VMEM),
-        out_shape=jax.ShapeDtypeStruct((2, 2, 8, 256, 2, 256), BF),
+        out_specs=[pl.BlockSpec(memory_space=pltpu.VMEM)] * 3,
+        out_shape=[
+            jax.ShapeDtypeStruct((3, 8, 256, 2, 256), BF),
+            jax.ShapeDtypeStruct((256, 512), BF),
+            jax.ShapeDtypeStruct((8, 512, 512), BF),
+        ],
         scratch_shapes=[
             pltpu.VMEM((4, 256, 512), BF),
-            pltpu.VMEM((2, 8, 512, 512), BF),
+            pltpu.VMEM((8, 512, 512), BF),
             pltpu.VMEM((2, 8, 32, 16, 128), BF),
             pltpu.VMEM((2, 1024, 256), BF),
             pltpu.VMEM((2, 512, 256), BF),
@@ -338,6 +380,22 @@
         ),
         name="transform",
     )(*far)
+    return pl.pallas_call(
+        finish_kernel,
+        in_specs=[pl.BlockSpec(memory_space=pltpu.VMEM)] * 3,
+        out_specs=anywhere,
+        out_shape=jax.ShapeDtypeStruct((2, 2, 8, 256, 2, 256), BF),
+        scratch_shapes=[
+            pltpu.VMEM((8, 256, 2, 256), BF),
+            pltpu.SemaphoreType.DMA((3,)),
+            pltpu.SemaphoreType.DMA((2,)),
+        ],
+        compiler_params=pltpu.CompilerParams(vmem_limit_bytes=26 << 20),
+        cost_estimate=pl.CostEstimate(
+            flops=2**30, bytes_accessed=8 << 20, transcendentals=0
+        ),
+        name="finish",
+    )(ready, last, left)
 
 
 def solution(mesh):

time: 45.3 us -> 43.6 us (0.962)
  local copies, waits for them, and re-layouts: 3.4 us -> 0 us
  Pallas kernels: 41.7 us -> 43.5 us
    unnamed x1 -> x0, local copies, waits for them, and re-layouts: 3.4 us -> none
    pallas_call x0 -> x1, Pallas kernels: none -> 3.34 us  [shards(): pl.pallas_call(finish_kernel, in_specs=[pl.BlockSpec(memory_space=pltpu.V...]
    pallas_call x1, Pallas kernels: 41.7 us -> 40.1 us  [shards(): pl.pallas_call(transform_kernel, in_specs=[pl.BlockSpec(memory_space=pltp...]
where the time goes in v7:
time: 43.6 us; the launch traced here: 43.5 us
  Pallas kernels  43.5 us (100%)
    pallas_call x1, Pallas kernels, shards(): pl.pallas_call(transform_kernel, in_specs=[pl.BlockSpec(memory_space=pltp...  40.1 us
    pallas_call x1, Pallas kernels, shards(): pl.pallas_call(finish_kernel, in_specs=[pl.BlockSpec(memory_space=pltpu.V...  3.34 us

profile of v7, /device:TPU:0, one launch (start us, length us, event | category | flops | bytes accessed | tf_op | source)
XLA Modules:
  0.0 43.5 jit_solution(4216396148516124352)
XLA Ops:
  0.0 40.1 %transform.1 = (bf16[3,8,256,2,256]{4,3,2,1,0:T(2,128)(2,1)S(1)}, bf16[256,512]{1,0:T(8,128)(2,1)S(1)}, bf16[8,512,512]{2,1,0:T(8,128)(2,1)S(1)}) custom-call(s32[2,256]{1,0:T(2,128)} %bitcast.1, s32[8]{0:T(128)} %offsets_ref.1, bf16[32,32,1024]{2,1,0:T(8,128)(2,1)} %x_hbm.1, bf16[1024,512]{1,0:T(8,128)(2,1)} %constant.4.table_hbm, bf16[2,512,256]{2,1,0:T(8,128)(2,1)} %proj_hbm.1), custom_call_target="tpu_custom_call" | custom-call | flops 4294967296 | bytes 12582912 | tf_op jit(solution)/shard_map/transform/pallas_call | solution.py:344
  40.1 3.3 %finish.1 = bf16[2,2,8,256,2,256]{5,4,3,2,1,0:T(2,128)(2,1)} custom-call(bf16[3,8,256,2,256]{4,3,2,1,0:T(2,128)(2,1)S(1)} %get-tuple-element.8.out_ref, bf16[256,512]{1,0:T(8,128)(2,1)S(1)} %get-tuple-element.9.last_ref, bf16[8,512,512]{2,1,0:T(8,128)(2,1)S(1)} %get-tuple-element.10.left_ref), custom_call_target="tpu_custom_call" | custom-call | flops 1073741824 | bytes 8388608 | tf_op jit(solution)/shard_map/finish/pallas_call | solution.py:383

commit v8 on v7

--- a/solution.py
+++ b/solution.py
@@ -164,12 +164,12 @@
                         up_ref[to_tm, to_lat] = v[slot]
                     else:
                         across_ref[to_lat, to_tm] = v[slot]
-    pl.semaphore_wait(barrier, 22 + outside.astype(jnp.int32))
-    for i in ACROSS[:8]:
-        across(i, across_ref.at[lat ^ i], via_across_ref.at[lat], 1).start()
-    for i in UP:
-        up(i, up_ref.at[tm ^ i], via_up_ref.at[tm], 0).start()
-    for i in ACROSS[8:]:
+        if bh == 0:
+            pl.semaphore_wait(barrier, 22 + outside.astype(jnp.int32))
+            for i in UP:
+                up(i, up_ref.at[tm ^ i], via_up_ref.at[tm], 0).start()
+
+    for i in ACROSS:
         across(i, across_ref.at[lat ^ i], via_across_ref.at[lat], 1).start()
     via_up_ref[tm] = up_ref[tm]
     via_across_ref[lat] = across_ref[lat]

time: 43.6 us -> 42.5 us (0.975)
  Pallas kernels: 43.5 us -> 42.4 us
    pallas_call x1, Pallas kernels: 40.1 us -> 39 us  [shards(): pl.pallas_call(transform_kernel, in_specs=[pl.BlockSpec(memory_space=pltp...]
where the time goes in v8:
time: 42.5 us; the launch traced here: 42.4 us
  Pallas kernels  42.4 us (100%)
    pallas_call x1, Pallas kernels, shards(): pl.pallas_call(transform_kernel, in_specs=[pl.BlockSpec(memory_space=pltp...  39 us
    pallas_call x1, Pallas kernels, shards(): pl.pallas_call(finish_kernel, in_specs=[pl.BlockSpec(memory_space=pltpu.V...  3.34 us

profile of v8, /device:TPU:0, one launch (start us, length us, event | category | flops | bytes accessed | tf_op | source)
XLA Modules:
  0.0 42.4 jit_solution(17656736790745380031)
XLA Ops:
  0.0 39.0 %transform.1 = (bf16[3,8,256,2,256]{4,3,2,1,0:T(2,128)(2,1)S(1)}, bf16[256,512]{1,0:T(8,128)(2,1)S(1)}, bf16[8,512,512]{2,1,0:T(8,128)(2,1)S(1)}) custom-call(s32[2,256]{1,0:T(2,128)} %bitcast.1, s32[8]{0:T(128)} %offsets_ref.1, bf16[32,32,1024]{2,1,0:T(8,128)(2,1)} %x_hbm.1, bf16[1024,512]{1,0:T(8,128)(2,1)} %constant.4.table_hbm, bf16[2,512,256]{2,1,0:T(8,128)(2,1)} %proj_hbm.1), custom_call_target="tpu_custom_call" | custom-call | flops 4294967296 | bytes 12582912 | tf_op jit(solution)/shard_map/transform/pallas_call | solution.py:344
  39.0 3.3 %finish.1 = bf16[2,2,8,256,2,256]{5,4,3,2,1,0:T(2,128)(2,1)} custom-call(bf16[3,8,256,2,256]{4,3,2,1,0:T(2,128)(2,1)S(1)} %get-tuple-element.8.out_ref, bf16[256,512]{1,0:T(8,128)(2,1)S(1)} %get-tuple-element.9.last_ref, bf16[8,512,512]{2,1,0:T(8,128)(2,1)S(1)} %get-tuple-element.10.left_ref), custom_call_target="tpu_custom_call" | custom-call | flops 1073741824 | bytes 8388608 | tf_op jit(solution)/shard_map/finish/pallas_call | solution.py:383

commit v9 on v8

--- a/solution.py
+++ b/solution.py
@@ -73,6 +73,7 @@
     via_across_ref,
     r_ref,
     a_ref,
+    part_ref,
     twice_ref,
     x_sem,
     table_sem,
@@ -176,7 +177,11 @@
 
     proj_copy.wait()
     for o in range(2):
-        flip_ref[o] = proj_ref[o].T
+        bands = proj_ref[o].reshape(16, 2, 16, 256)
+        for half in range(2):
+            flip_ref[o, :, 256 * half : 256 * half + 256] = (
+                bands[:, half].reshape(256, 256).T
+            )
 
     some = pl.ds(0, 7)
     up_all = up(0, up_ref.at[some], via_up_ref.at[some], 0)
@@ -201,12 +206,18 @@
         else:
             up_last.wait_recv()
         for i in range(16):
-            rows = slice(32 * i + 16 * half, 32 * i + 16 * half + 16)
+            rows = slice(256 * half + 16 * i, 256 * half + 16 * i + 16)
             for q in range(2):
                 v = [r_ref[4 * q + j, i, half] for j in range(4)]
                 v = swap_index_and_lanes(v, 32)
                 for op in range(4):
                     a_ref[op // 2, 2 * (op % 2) + q, rows, :] = v[op]
+        if half == 0:
+            for o in range(2):
+                columns = jnp.concatenate([a_ref[o, j, :256] for j in range(4)], axis=1)
+                part_ref[o] = jnp.dot(
+                    flip_ref[o, :, :256], columns, preferred_element_type=F32
+                )
     degree = lax.broadcasted_iota(jnp.int32, (256, 512), 0)
     before = jnp.maximum(me - 1, 0)
 
@@ -221,8 +232,10 @@
         )
 
     for o in range(2):
-        columns = jnp.concatenate([a_ref[o, j] for j in range(4)], axis=1)
-        h = jnp.dot(flip_ref[o], columns, preferred_element_type=F32)
+        columns = jnp.concatenate([a_ref[o, j, 256:] for j in range(4)], axis=1)
+        h = part_ref[o] + jnp.dot(
+            flip_ref[o, :, 256:], columns, preferred_element_type=F32
+        )
         low, high = range_ref[0, 2 * me + o], range_ref[1, 2 * me + o]
         keep = (degree >= low) & (degree < high)
         h_ref[o] = jnp.where(keep, h, 0.0).astype(BF)
@@ -363,6 +376,7 @@
             pltpu.VMEM((16, 8, 16, 128), BF),
             pltpu.VMEM((8, 16, 2, 16, 128), BF),
             pltpu.VMEM((2, 4, 512, 128), BF),
+            pltpu.VMEM((2, 256, 512), F32),
             pltpu.VMEM((2, 512, 512), F32),
             pltpu.SemaphoreType.DMA((2, 8)),
             pltpu.SemaphoreType.DMA((2,)),

time: 42.5 us -> 42.4 us (level)
  no operation moved by 1% of the time
where the time goes in v9:
time: 42.4 us; the launch traced here: 42.2 us
  Pallas kernels  42.2 us (100%)
    pallas_call x1, Pallas kernels, shards(): pl.pallas_call(transform_kernel, in_specs=[pl.BlockSpec(memory_space=pltp...  38.9 us
    pallas_call x1, Pallas kernels, shards(): pl.pallas_call(finish_kernel, in_specs=[pl.BlockSpec(memory_space=pltpu.V...  3.34 us

profile of v9, /device:TPU:0, one launch (start us, length us, event | category | flops | bytes accessed | tf_op | source)
XLA Modules:
  0.0 42.2 jit_solution(8928269192547829742)
XLA Ops:
  0.0 38.9 %transform.1 = (bf16[3,8,256,2,256]{4,3,2,1,0:T(2,128)(2,1)S(1)}, bf16[256,512]{1,0:T(8,128)(2,1)S(1)}, bf16[8,512,512]{2,1,0:T(8,128)(2,1)S(1)}) custom-call(s32[2,256]{1,0:T(2,128)} %bitcast.1, s32[8]{0:T(128)} %offsets_ref.1, bf16[32,32,1024]{2,1,0:T(8,128)(2,1)} %x_hbm.1, bf16[1024,512]{1,0:T(8,128)(2,1)} %constant.4.table_hbm, bf16[2,512,256]{2,1,0:T(8,128)(2,1)} %proj_hbm.1), custom_call_target="tpu_custom_call" | custom-call | flops 4294967296 | bytes 12582912 | tf_op jit(solution)/shard_map/transform/pallas_call | solution.py:357
  38.9 3.3 %finish.1 = bf16[2,2,8,256,2,256]{5,4,3,2,1,0:T(2,128)(2,1)} custom-call(bf16[3,8,256,2,256]{4,3,2,1,0:T(2,128)(2,1)S(1)} %get-tuple-element.8.out_ref, bf16[256,512]{1,0:T(8,128)(2,1)S(1)} %get-tuple-element.9.last_ref, bf16[8,512,512]{2,1,0:T(8,128)(2,1)S(1)} %get-tuple-element.10.left_ref), custom_call_target="tpu_custom_call" | custom-call | flops 1073741824 | bytes 8388608 | tf_op jit(solution)/shard_map/finish/pallas_call | solution.py:397
